TPU v7x, 128 devices: a whole 4x4x4 slice. The times are simulated.
128 devices in a mesh: dp: 1, tp: 16 (over z, y), fsdp: 8 (over x, core).
Axes of the slice: x: 4, y: 4, z: 4, core: 2. Of those that a mesh axis runs over, the one named last changes fastest.
Arguments:
- hidden: bfloat16 [8, 2048, 4096], P(('dp', 'fsdp'))
- positions: int32 [2048], replicated
- norm_gain: float32 [4096], P('fsdp')
- w_query: bfloat16 [4096, 4096], P('fsdp', 'tp')
- w_key: bfloat16 [4096, 256], P('fsdp')
- w_value: bfloat16 [4096, 256], P('fsdp')
- w_gate: bfloat16 [4096, 16384], P('fsdp', 'tp')
- w_up: bfloat16 [4096, 16384], P('fsdp', 'tp')
- w_out: bfloat16 [4096, 4096], P('tp', 'fsdp')
- w_down: bfloat16 [16384, 4096], P('tp', 'fsdp')
Outputs:
- output: bfloat16 [8, 2048, 4096], P(('dp', 'fsdp'))
All inputs are finite; a program needn't handle non-finite values.
Results may differ from a plain program's by a relative error of at most 0.0110866.
Values are sent between devices in bfloat16 or wider.
A program may use at most 1 GiB of HBM per device.

v0:
```python
import jax
import jax.numpy as jnp
from jax import lax
from jax.sharding import PartitionSpec as P

Q_BLOCK = 512
NORM_EPS = 1e-6


def rope_tables(positions, head_dim):
    inv_freq = 10000.0 ** (-jnp.arange(0, head_dim, 2, dtype=jnp.float32) / head_dim)
    angles = positions.astype(jnp.float32)[:, None] * inv_freq[None, :]
    angles = jnp.concatenate([angles, angles], axis=-1)
    return jnp.cos(angles), jnp.sin(angles)


def rope_rotate(vectors, cos_t, sin_t):
    half_dim = vectors.shape[-1] // 2
    rotated = jnp.concatenate([-vectors[..., half_dim:], vectors[..., :half_dim]], axis=-1)
    return vectors * cos_t + rotated * sin_t


def layer_norm(hidden, gain_vec):
    row_f32 = hidden.astype(jnp.float32)
    centered = row_f32 - jnp.mean(row_f32, axis=-1, keepdims=True)
    variance = jnp.mean(centered * centered, axis=-1, keepdims=True)
    return (centered * lax.rsqrt(variance + NORM_EPS) * gain_vec).astype(jnp.bfloat16)


def project(operand, weight):
    return jnp.einsum("bsn,nm->bsm", operand, weight, preferred_element_type=jnp.float32)


def causal_attention(query_rot, key_rot, values):
    batch = query_rot.shape[0]
    seq_len = query_rot.shape[1]
    n_heads = query_rot.shape[2]
    head_dim = query_rot.shape[3]
    q_block = min(Q_BLOCK, seq_len)
    score_scale = head_dim ** -0.5
    pieces = []
    for blk_idx in range(seq_len // q_block):
        blk_lo = blk_idx * q_block
        blk_hi = blk_lo + q_block
        scores = jnp.einsum("bshe,bte->bsht", query_rot[:, blk_lo:blk_hi], key_rot[:, :blk_hi], preferred_element_type=jnp.float32) * score_scale
        causal_mask = jnp.arange(blk_hi)[None, :] <= (blk_lo + jnp.arange(q_block))[:, None]
        scores = jnp.where(causal_mask[None, :, None, :], scores, -1e30)
        prob_rows = jax.nn.softmax(scores, axis=-1).astype(jnp.bfloat16)
        pieces.append(jnp.einsum("bsht,bte->bshe", prob_rows, values[:, :blk_hi], preferred_element_type=jnp.float32).astype(jnp.bfloat16))
    attn_out = jnp.concatenate(pieces, axis=1)
    return attn_out.reshape(batch, seq_len, n_heads * head_dim)


def solution(mesh):
    row_spec = P(("dp", "fsdp"), None, None)

    def local_layer(hidden, positions, norm_gain, w_query, w_key, w_value, w_gate, w_up, w_out, w_down):
        gain_full = lax.all_gather(norm_gain, "fsdp", axis=0, tiled=True)
        wq_full = lax.all_gather(w_query, "fsdp", axis=0, tiled=True)
        wk_full = lax.all_gather(w_key, "fsdp", axis=0, tiled=True)
        wv_full = lax.all_gather(w_value, "fsdp", axis=0, tiled=True)
        wg_full = lax.all_gather(w_gate, "fsdp", axis=0, tiled=True)
        wu_full = lax.all_gather(w_up, "fsdp", axis=0, tiled=True)
        wo_full = lax.all_gather(w_out, "fsdp", axis=1, tiled=True)
        wd_full = lax.all_gather(w_down, "fsdp", axis=1, tiled=True)
        batch = hidden.shape[0]
        seq_len = hidden.shape[1]
        head_dim = wk_full.shape[1]
        normed = layer_norm(hidden, gain_full)
        query_raw = project(normed, wq_full).astype(jnp.bfloat16)
        key_raw = project(normed, wk_full).astype(jnp.bfloat16)
        values = project(normed, wv_full).astype(jnp.bfloat16)
        gate_raw = project(normed, wg_full).astype(jnp.bfloat16)
        up_raw = project(normed, wu_full).astype(jnp.bfloat16)
        cos_t, sin_t = rope_tables(positions, head_dim)
        query_rot = rope_rotate(query_raw.reshape(batch, seq_len, -1, head_dim).astype(jnp.float32), cos_t[:, None, :], sin_t[:, None, :]).astype(jnp.bfloat16)
        key_rot = rope_rotate(key_raw.astype(jnp.float32), cos_t, sin_t).astype(jnp.bfloat16)
        attn_out = causal_attention(query_rot, key_rot, values)
        gated_act = (jax.nn.silu(gate_raw.astype(jnp.float32)) * up_raw.astype(jnp.float32)).astype(jnp.bfloat16)
        branch = project(attn_out, wo_full) + project(gated_act, wd_full)
        branch = lax.psum(branch.astype(jnp.bfloat16), "tp")
        return (hidden.astype(jnp.float32) + branch.astype(jnp.float32)).astype(jnp.bfloat16)

    in_specs = (row_spec, P(None), P("fsdp"), P("fsdp", "tp"), P("fsdp", None), P("fsdp", None), P("fsdp", "tp"), P("fsdp", "tp"), P("tp", "fsdp"), P("tp", "fsdp"))
    return jax.shard_map(local_layer, mesh=mesh, in_specs=in_specs, out_specs=row_spec, check_vma=False)
```

profile of v0, /device:TPU:0, one launch (start us, length us, event | category | flops | bytes accessed | tf_op | source)
XLA Modules:
  0.0 568.0 jit_solution(14693293102553778612)
XLA Ops:
  6.5 0.7 all-gather.9.cloned.1.call-update
  7.3 0.7 all-gather.11.cloned.1.call-update
  8.1 0.7 all-gather.13.cloned.1.call-update
  8.8 0.5 all-gather.15.cloned.1.call-update
  9.4 0.5 all-gather.17.cloned.1.call-update
  10.0 0.5 all-gather.19.cloned.1.call-update
  10.5 0.7 all-gather.21.cloned.1.call-update
  11.4 7.0 %convert_reduce_fusion = f32[2048]{0:T(1024)S(1)} fusion(bf16[1,2048,4096]{2,1,0:T(8,128)(2,1)} %param.10), kind=kLoop, calls=%fused_computation.2 | loop fusion | flops 16775168 | bytes 16785408 | tf_op jit(solution)/shard_map/reduce_sum | solution.py:25
  18.4 3.6 copy-done
  22.0 5.8 %fusion.2 = f32[2048]{0:T(1024)S(1)} fusion(bf16[1,2048,4096]{2,1,0:T(8,128)(2,1)S(1)} %copy-done, f32[2048]{0:T(1024)S(1)} %broadcast_multiply_fusion.1), kind=kLoop, calls=%fused_computation.5 | loop fusion | flops 33552384 | bytes 16793600 | tf_op jit(solution)/shard_map/reduce_sum | solution.py:26
  27.8 13.2 %all-gather = f32[8,1,512]{2,1,0:T(1,128)S(1)} all-gather(f32[1,1,512]{2,1,0:T(1,128)S(1)} %bitcast.99), channel_id=1, replica_groups=mesh['dp'=1,'tp'=16,'fsdp'=8] {'fsdp'}, dimensions={0}, use_global_device_ids=true | all-gather | bytes 18432 | tf_op jit(solution)/shard_map/all_gather | solution.py:58
  41.0 0.1 broadcast_multiply_fusion
  41.2 10.3 %fusion.6 = bf16[2048,4096]{1,0:T(8,128)(2,1)} fusion(bf16[1,2048,4096]{2,1,0:T(8,128)(2,1)S(1)} %copy-done, f32[4096]{0:T(1024)S(1)} %bitcast.98, f32[2048]{0:T(1024)S(1)} %add_rsqrt_fusion, f32[2048]{0:T(1024)S(1)} %broadcast_multiply_fusion.1), kind=kLoop, calls=%fused_computation.10 | loop fusion | flops 41943040 | bytes 33587200 | tf_op jit(solution)/shard_map/reshape.5
  51.5 10.9 %convolution_convert_fusion.1 = bf16[2048,256]{0,1:T(8,128)(2,1)S(1)} fusion(bf16[2048,4096]{1,0:T(8,128)(2,1)} %fusion.6, bf16[4096,256]{1,0:T(8,128)(2,1)} %all-gather.9.cloned.1.call-done), kind=kOutput, calls=%fused_computation.35 | convolution fusion | flops 4295491584 | bytes 19922944 | tf_op jit(solution)/shard_map/bsn,nm->bsm/dot_general | solution.py:31
  62.4 0.2 convert_bitcast_fusion.1
  62.6 1.5 fusion.37
  64.1 10.9 %convolution_convert_fusion = bf16[2048,256]{0,1:T(8,128)(2,1)S(1)} fusion(bf16[2048,4096]{1,0:T(8,128)(2,1)} %fusion.6, bf16[4096,256]{1,0:T(8,128)(2,1)} %all-gather.11.cloned.1.call-done), kind=kOutput, calls=%fused_computation.34 | convolution fusion | flops 4295491584 | bytes 19922944 | tf_op jit(solution)/shard_map/bsn,nm->bsm/dot_general | solution.py:31
  75.0 0.2 convert_bitcast_fusion
  75.2 0.2 fusion.36
  75.4 0.7 copy-done.2
  76.2 0.3 copy-done.3
  76.5 8.5 %fusion.45 = (bf16[1,2048,1,256]{1,3,2,0:T(8,128)(2,1)S(1)}, bf16[2048,256]{0,1:T(8,128)(2,1)S(1)}) fusion(f32[2048,128]{0,1:T(8,128)S(1)} %copy-done.3, f32[2048,128]{0,1:T(8,128)S(1)} %copy-done.2, f32[2048,128]{0,1:T(8,128)S(1)} %broadcast_multiply_fusion, bf16[2048,256]{0,1:T(8,128)(2,1)S(1)} %convolution_convert_fusion.1, ...), kind=kLoop, calls=%fused_computation.78 | loop fusion | flops 6815744 | bytes 9437184 | tf_op jit(solution)/shard_map/convert_element_type | solution.py:76
  85.0 1.0 copy-done.5
  85.9 0.3 copy-done.7
  86.3 2.8 multiply_select_fusion
  89.0 2.4 all-gather.13.cloned.1.call-done
  91.4 12.4 %fusion.52 = f32[2048,256]{1,0:T(8,128)} fusion(bf16[2048,4096]{1,0:T(8,128)(2,1)} %fusion.6, bf16[4096,256]{1,0:T(8,128)(2,1)} %all-gather.13.cloned.1.call-done), kind=kOutput, calls=%fused_computation.103 | convolution fusion | flops 4294967296 | bytes 20971520 | tf_op jit(solution)/shard_map/bsn,nm->bsm/dot_general | solution.py:31
  103.8 4.5 online-softmax
  108.4 0.4 fusion.51
  108.7 0.2 fusion.46
  108.9 0.6 fusion.50
  109.6 0.5 fusion.29
  110.1 0.9 fusion.49
  111.0 0.6 fusion.18
  111.6 0.1 copy-done.1
  111.7 0.1 convert_bitcast_fusion.2
  111.8 0.4 fusion.33
  112.2 0.6 fusion.34
  112.8 0.7 fusion.35
  113.5 5.2 all-gather.15.cloned.1.call-done
  118.7 16.2 %fusion.38 = f32[2048,4096]{1,0:T(8,128)} fusion(bf16[256,4096]{1,0:T(8,128)(2,1)} %all-gather.15.cloned.1.call-done, bf16[1,512,1,256]{3,1,2,0:T(8,128)(2,1)S(1)} %convert_bitcast_fusion.3, bf16[1,512,1,256]{3,1,2,0:T(8,128)(2,1)S(1)} %fusion.35, bf16[1,512,1,256]{3,1,2,0:T(8,128)(2,1)S(1)} %fusion.34, bf16[1,512,1,256]{3,1,2,0:T(8,128)(2,1)S(1)} %fusion.33), kind=kOutput, calls=%fused_computation.67 | convolution fusion | flops 4299161600 | bytes 36700160 | tf_op jit(solution)/shard_map/bsn,nm->bsm/dot_general | solution.py:31
  134.8 35.5 %all-gather.17.cloned.1.call-done = bf16[4096,1024]{1,0:T(8,128)(2,1)} async-done(((bf16[512,1024]{1,0:T(8,128)(2,1)}), bf16[4096,1024]{1,0:T(8,128)(2,1)}) %all-gather.17.cloned.1.call-update) | async-done | bytes 8388624 | tf_op jit(solution)/shard_map/all_gather | solution.py:62
  170.4 23.7 %fusion.53 = bf16[2048,1024]{1,0:T(8,128)(2,1)} fusion(bf16[2048,4096]{1,0:T(8,128)(2,1)} %fusion.6, bf16[4096,1024]{1,0:T(8,128)(2,1)} %all-gather.17.cloned.1.call-done), kind=kOutput, calls=%fused_computation.104 | convolution fusion | flops 17179869184 | bytes 29360128 | tf_op jit(solution)/shard_map/bsn,nm->bsm/dot_general | solution.py:31
  194.0 27.7 %all-gather.19.cloned.1.call-done = bf16[4096,1024]{1,0:T(8,128)(2,1)} async-done(((bf16[512,1024]{1,0:T(8,128)(2,1)}), bf16[4096,1024]{1,0:T(8,128)(2,1)}) %all-gather.19.cloned.1.call-update) | async-done | bytes 8388624 | tf_op jit(solution)/shard_map/all_gather | solution.py:63
  221.7 51.5 %all-gather.21.cloned.1.call-done = bf16[1024,4096]{1,0:T(8,128)(2,1)} async-done(((bf16[1024,512]{1,0:T(8,128)(2,1)}), bf16[1024,4096]{1,0:T(8,128)(2,1)}) %all-gather.21.cloned.1.call-update) | async-done | bytes 8388624 | tf_op jit(solution)/shard_map/all_gather | solution.py:65
  273.2 47.5 %fusion.7 = bf16[1,2048,4096]{2,1,0:T(8,128)(2,1)} fusion(f32[2048,4096]{1,0:T(8,128)} %fusion.38, bf16[1024,4096]{1,0:T(8,128)(2,1)} %all-gather.21.cloned.1.call-done, bf16[2048,1024]{1,0:T(8,128)(2,1)} %fusion.53, bf16[2048,4096]{1,0:T(8,128)(2,1)} %fusion.6, bf16[4096,1024]{1,0:T(8,128)(2,1)} %all-gather.19.cloned.1.call-done), kind=kOutput, calls=%fused_computation.11 | convolution fusion | flops 34395389952 | bytes 88080384 | tf_op jit(solution)/shard_map/bsn,nm->bsm/dot_general | solution.py:31
  320.7 220.7 %all-reduce.2.cloned.1.call-done = bf16[1,2048,4096]{2,1,0:T(8,128)(2,1)} async-done(((bf16[1,2048,4096]{2,1,0:T(8,128)(2,1)}), bf16[1,2048,4096]{2,1,0:T(8,128)(2,1)}) %all-reduce.2.cloned.1.call-update) | async-done | bytes 16777232 | tf_op jit(solution)/shard_map/psum | solution.py:81
  541.4 19.3 %fusion.5 = bf16[1,2048,4096]{2,1,0:T(8,128)(2,1)} fusion(bf16[1,2048,4096]{2,1,0:T(8,128)(2,1)} %param.10, bf16[1,2048,4096]{2,1,0:T(8,128)(2,1)} %all-reduce.2.cloned.1.call-done), kind=kLoop, calls=%fused_computation.8 | loop fusion | flops 33554432 | bytes 50331648 | tf_op jit(solution)/shard_map/convert_element_type | solution.py:82
  (35 shorter events, 0.4 us)
Async XLA Ops:
  6.5 4.8 copy-start.9
  6.5 44.9 %all-gather.9.cloned.1.call-start = ((), (), s32[]{:S(2)}) async-start(), calls=%async_computation | async-start | bytes 2359296 | tf_op jit(solution)/shard_map/all_gather | solution.py:59
  7.3 56.8 %all-gather.11.cloned.1.call-start = ((), (), s32[]{:S(2)}) async-start(), calls=%async_computation.1 | async-start | bytes 2359296 | tf_op jit(solution)/shard_map/all_gather | solution.py:60
  8.0 83.4 %all-gather.13.cloned.1.call-start = ((), (), s32[]{:S(2)}) async-start(), calls=%async_computation.2 | async-start | bytes 2359296 | tf_op jit(solution)/shard_map/all_gather | solution.py:61
  8.7 109.9 %all-gather.15.cloned.1.call-start = ((), (), s32[]{:S(2)}) async-start(), calls=%async_computation.3 | async-start | bytes 2359296 | tf_op jit(solution)/shard_map/all_gather | solution.py:64
  9.3 161.1 %all-gather.17.cloned.1.call-start = ((), (), s32[]{:S(2)}) async-start(), calls=%async_computation.4 | async-start | bytes 9437184 | tf_op jit(solution)/shard_map/all_gather | solution.py:62
  9.9 211.8 %all-gather.19.cloned.1.call-start = ((), (), s32[]{:S(2)}) async-start(), calls=%async_computation.5 | async-start | bytes 9437184 | tf_op jit(solution)/shard_map/all_gather | solution.py:63
  10.5 262.7 %all-gather.21.cloned.1.call-start = ((), (), s32[]{:S(2)}) async-start(), calls=%async_computation.6 | async-start | bytes 9437184 | tf_op jit(solution)/shard_map/all_gather | solution.py:65
  11.2 530.2 %all-reduce.2.cloned.1.call-start = ((), (), s32[]{:S(2)}) async-start(), calls=%async_computation.7 | async-start | bytes 33554432 | tf_op jit(solution)/shard_map/psum | solution.py:81
  11.3 10.7 %copy-start = (bf16[1,2048,4096]{2,1,0:T(8,128)(2,1)S(1)}, bf16[1,2048,4096]{2,1,0:T(8,128)(2,1)}, u32[]{:S(2)}) copy-start(bf16[1,2048,4096]{2,1,0:T(8,128)(2,1)} %param.10) | copy-start | bytes 50331652
  22.0 5.8 %copy-start.10 = (f32[512]{0:T(512)S(1)}, f32[512]{0:T(512)}, u32[]{:S(2)}) copy-start(f32[512]{0:T(512)} %param.12) | copy-start | bytes 6148
  75.0 1.2 copy-start.2
  75.0 1.5 copy-start.3
  85.0 1.0 copy-start.5
  85.0 1.3 copy-start.7
  103.8 4.5 copy-start.6
  103.8 4.5 copy-start.8
  108.9 1.1 copy-start.4
  110.1 1.6 copy-start.1
Sparse Core Ops, SparseCore 0:
  9.0 27.5 all-gather.8
  38.3 25.6 all-gather.10
  65.7 25.6 all-gather.12
  93.0 25.6 all-gather.14
  120.2 50.0 all-gather.16
  172.0 49.7 all-gather.18
  223.4 49.7 all-gather.20
  320.8 220.5 all-reduce.1
where the time goes:
time: 577 us; the launch traced here: 568 us
  waiting for transfers between devices  347 us (60%)
  matrix products  128 us (22%)
  other arithmetic  54.6 us (9%)
  between operations  14.2 us (2%)
  blocking collectives  13.2 us (2%)
  local copies, waits for them, and re-layouts  6.12 us (1%)
    psum x1, waiting for transfers between devices, local_layer(): branch = lax.psum(branch.astype(jnp.bfloat16), 'tp')  221 us
    dot_general x6, matrix products, project(): jnp.einsum('bsn,nm->bsm', operand, weight, preferred_element_type=jnp.flo...  121 us
    all_gather x1, waiting for transfers between devices, local_layer(): wd_full = lax.all_gather(w_down, 'fsdp', axis=1, tiled=True)  51.5 us
    all_gather x1, waiting for transfers between devices, local_layer(): wg_full = lax.all_gather(w_gate, 'fsdp', axis=0, tiled=True)  35.5 us
    all_gather x1, waiting for transfers between devices, local_layer(): wu_full = lax.all_gather(w_up, 'fsdp', axis=0, tiled=True)  27.7 us
    convert_element_type x1, other arithmetic, local_layer(): (hidden.astype(jnp.float32) + branch.astype(jnp.float32)).astype(jnp.bflo...  19.3 us
    all_gather x1, blocking collectives, local_layer(): gain_full = lax.all_gather(norm_gain, 'fsdp', axis=0, tiled=True)  13.2 us
  transfers between devices with their start and end apart: 8, of which 6 were waited for; matrix products, arithmetic and copies ran while one was open for 20% of the time, Pallas kernels for 1%

commit v1 on v0

--- a/solution.py
+++ b/solution.py
@@ -1,6 +1,8 @@
 import jax
 import jax.numpy as jnp
 from jax import lax
+from jax.experimental import pallas as pl
+from jax.experimental.pallas import tpu as pltpu
 from jax.sharding import PartitionSpec as P
 
 Q_BLOCK = 512
@@ -51,35 +53,329 @@
     return attn_out.reshape(batch, seq_len, n_heads * head_dim)
 
 
+MESH = pl.DeviceIdType.MESH
+TPA = 4
+COL = 8
+
+
+def _ring_ids(t):
+    z, y = t // TPA, t % TPA
+    y_r, y_l = z * TPA + (y + 1) % TPA, z * TPA + (y + 3) % TPA
+    z_r, z_l = ((z + 1) % TPA) * TPA + y, ((z + 3) % TPA) * TPA + y
+    return (y, y_r, y_l), (z, z_r, z_l)
+
+
+def _fsdp_ids(f):
+    xc, core = f // 2, f % 2
+    f_p = xc * 2 + (1 - core)
+    f_r = ((xc + 1) % 4) * 2 + core
+    f_l = ((xc + 3) % 4) * 2 + core
+    return xc, core, f_p, f_r, f_l
+
+
+def reduce_kernel(az, x_hbm, wo, wd, out, wbuf, part, r1, r2, r3, r4, ybuf, xbuf,
+                  ssem, rsem, wss, wrs, lsem, osem):
+    t = lax.axis_index("tp")
+    f = lax.axis_index("fsdp")
+    ring_y, ring_z = _ring_ids(t)
+    xc, core, f_p, f_r, f_l = _fsdp_ids(f)
+    seq = az.shape[0]
+    cols = wbuf.shape[2]
+    half = seq // 2
+    big = half // TPA
+    small = big // TPA
+    hd = wo.shape[0]
+
+    ld_o = pltpu.make_async_copy(wo, wbuf.at[0, pl.ds(0, hd)], lsem.at[0])
+    ld_d = pltpu.make_async_copy(wd, wbuf.at[0, pl.ds(hd, wd.shape[0])], lsem.at[1])
+    ld_o.start()
+    ld_d.start()
+    axes = ((ring_y, ring_z), (ring_z, ring_y))
+
+    def own_rows(h):
+        (i1, _, _), (i2, _, _) = axes[h]
+        return pl.multiple_of(h * half + i1 * big + i2 * small, small)
+
+    ld_x = [pltpu.make_async_copy(x_hbm.at[pl.ds(own_rows(h), small), :], xbuf.at[h], lsem.at[2 + h]) for h in range(2)]
+    for c in ld_x:
+        c.start()
+
+    barrier = pltpu.get_barrier_semaphore()
+    for other in (ring_y[1], ring_y[2], ring_z[1], ring_z[2]):
+        pl.semaphore_signal(barrier, inc=1, device_id={"tp": other}, device_id_type=MESH)
+    for other in (f_p, f_r, f_l):
+        pl.semaphore_signal(barrier, inc=1, device_id={"fsdp": other}, device_id_type=MESH)
+    pl.semaphore_wait(barrier, 7)
+
+    def wcopy(k, src, dst, dev):
+        return pltpu.make_async_remote_copy(src_ref=src, dst_ref=dst, send_sem=wss.at[k], recv_sem=wrs.at[k],
+                                            device_id={"fsdp": dev}, device_id_type=MESH)
+
+    kk = wbuf.shape[1]
+    kh = kk // 2
+    top, bot = pl.ds(0, kh), pl.ds(kh, kh)
+    w_own_p = wcopy(0, wbuf.at[0], wbuf.at[1], f_p)
+    w_own_r = wcopy(1, wbuf.at[0], wbuf.at[2], f_r)
+    w_own_l = wcopy(2, wbuf.at[0], wbuf.at[4], f_l)
+    w_2p = wcopy(3, wbuf.at[2], wbuf.at[3], f_p)
+    w_4p = wcopy(4, wbuf.at[4], wbuf.at[5], f_p)
+    w_2r = wcopy(5, wbuf.at[2, top], wbuf.at[6, top], f_r)
+    w_4l = wcopy(6, wbuf.at[4, bot], wbuf.at[6, bot], f_l)
+    w_6p = wcopy(7, wbuf.at[6], wbuf.at[7], f_p)
+    ld_o.wait()
+    ld_d.wait()
+    w_own_r.start()
+    w_own_l.start()
+    w_own_p.start()
+    for c in ld_x:
+        c.wait()
+
+    def block_of(k):
+        q = k // 2
+        dx = 3 * q - 5 * (q // 2) - 2 * (q // 3)
+        return ((xc + dx) % 4) * 2 + (core + k % 2) % 2
+
+    def ring_copy(cb, h, d, step, src, dst, dev):
+        return pltpu.make_async_remote_copy(src_ref=src, dst_ref=dst, send_sem=ssem.at[cb, h, d, step],
+                                            recv_sem=rsem.at[cb, h, d, step], device_id={"tp": dev}, device_id_type=MESH)
+
+    def rs_first(cb, h, step, ring, base, n, land):
+        i, r, l = ring
+        o = (i + 2) % TPA
+        m = n // 2
+        s = pl.multiple_of(base + o * n, m)
+        return (ring_copy(cb, h, 0, step, part.at[cb, pl.ds(s, m)], land.at[cb, h, 0], r),
+                ring_copy(cb, h, 1, step, part.at[cb, pl.ds(s + m, m)], land.at[cb, h, 1], l))
+
+    def rs_second(cb, h, step, ring, base, n, land):
+        i, r, l = ring
+        s_r = pl.multiple_of(base + ((i + 1) % TPA) * n, n)
+        s_l = pl.multiple_of(base + ((i + 3) % TPA) * n, n)
+        return (ring_copy(cb, h, 0, step, part.at[cb, pl.ds(s_r, n)], land.at[cb, h, 0], r),
+                ring_copy(cb, h, 1, step, part.at[cb, pl.ds(s_l, n)], land.at[cb, h, 1], l))
+
+    def rs_update(cb, h, ring, base, n, land):
+        i, _, _ = ring
+        m = n // 2
+        s_r = pl.multiple_of(base + ((i + 1) % TPA) * n, m)
+        s_l = pl.multiple_of(base + ((i + 3) % TPA) * n + m, m)
+        for s, d in ((s_r, 0), (s_l, 1)):
+            rows = pl.ds(s, m)
+            part[cb, rows] = (part[cb, rows].astype(jnp.float32) + land[cb, h, d].astype(jnp.float32)).astype(jnp.bfloat16)
+
+    def ag_first(cb, h, step, ring, src, base, n):
+        i, r, l = ring
+        g = block_of(cb)
+        dst = out.at[g, pl.ds(pl.multiple_of(base + i * n, n), n)]
+        if src is None:
+            src = dst
+        return (ring_copy(cb, h, 0, step, src, dst, r), ring_copy(cb, h, 1, step, src, dst, l))
+
+    def ag_second(cb, h, step, ring, base, n):
+        i, r, l = ring
+        g = block_of(cb)
+        m = n // 2
+        from_l = out.at[g, pl.ds(pl.multiple_of(base + ((i + 3) % TPA) * n, m), m)]
+        from_r = out.at[g, pl.ds(pl.multiple_of(base + ((i + 1) % TPA) * n + m, m), m)]
+        return (ring_copy(cb, h, 0, step, from_l, from_l, r), ring_copy(cb, h, 1, step, from_r, from_r, l))
+
+    def copies(cb, step):
+        res = []
+        for h in range(2):
+            ring1, ring2 = axes[h]
+            base1 = h * half
+            base2 = pl.multiple_of(h * half + ring1[0] * big, big)
+            if step == 0:
+                res.extend(rs_first(cb, h, step, ring1, base1, big, r1))
+            elif step == 1:
+                res.extend(rs_second(cb, h, step, ring1, base1, big, r2))
+            elif step == 2:
+                res.extend(rs_first(cb, h, step, ring2, base2, small, r3))
+            elif step == 3:
+                res.extend(rs_second(cb, h, step, ring2, base2, small, r4))
+            elif step == 4:
+                res.extend(ag_first(cb, h, step, ring2, ybuf.at[cb, h], base2, small))
+            elif step == 5:
+                res.extend(ag_second(cb, h, step, ring2, base2, small))
+            elif step == 6:
+                res.extend(ag_first(cb, h, step, ring1, None, base1, big))
+            else:
+                res.extend(ag_second(cb, h, step, ring1, base1, big))
+        return res
+
+    def start(cb, step):
+        for c in copies(cb, step):
+            c.start()
+
+    def finish(cb, step):
+        for c in copies(cb, step):
+            c.wait_recv()
+            c.wait_send()
+
+    def own_out(cb, h):
+        return pltpu.make_async_copy(ybuf.at[cb, h], out.at[block_of(cb), pl.ds(own_rows(h), small)], osem.at[cb, h])
+
+    def stage0(cb):
+        @pl.when(cb == 1)
+        def _():
+            w_own_p.wait()
+
+        @pl.when(cb == 2)
+        def _():
+            w_own_r.wait()
+            w_own_l.wait()
+            w_2r.start()
+            w_4l.start()
+            w_2p.start()
+            w_4p.start()
+
+        @pl.when(cb == 3)
+        def _():
+            w_2p.wait()
+
+        @pl.when(cb == 5)
+        def _():
+            w_4p.wait()
+
+        @pl.when(cb == 6)
+        def _():
+            w_2r.wait()
+            w_4l.wait()
+            w_6p.start()
+
+        @pl.when(cb == 7)
+        def _():
+            w_6p.wait()
+
+        @pl.loop(0, seq // MT)
+        def _(i):
+            rows = pl.ds(pl.multiple_of(i * MT, MT), MT)
+            part[cb, rows] = jnp.dot(az[rows, :], wbuf[cb], preferred_element_type=jnp.float32).astype(jnp.bfloat16)
+
+        start(cb, 0)
+
+    def stage1(cb):
+        finish(cb, 0)
+        for h in range(2):
+            rs_update(cb, h, axes[h][0], h * half, big, r1)
+        start(cb, 1)
+
+    def stage2(cb):
+        finish(cb, 1)
+        for h in range(2):
+            rows = pl.ds(pl.multiple_of(h * half + axes[h][0][0] * big, big), big)
+            part[cb, rows] = (part[cb, rows].astype(jnp.float32) + r2[cb, h, 0].astype(jnp.float32)
+                              + r2[cb, h, 1].astype(jnp.float32)).astype(jnp.bfloat16)
+        start(cb, 2)
+
+    def stage3(cb):
+        finish(cb, 2)
+        for h in range(2):
+            rs_update(cb, h, axes[h][1], pl.multiple_of(h * half + axes[h][0][0] * big, big), small, r3)
+        start(cb, 3)
+
+    def stage4(cb):
+        finish(cb, 3)
+        g = block_of(cb)
+        for h in range(2):
+            branch = (part[cb, pl.ds(own_rows(h), small)].astype(jnp.float32) + r4[cb, h, 0].astype(jnp.float32)
+                      + r4[cb, h, 1].astype(jnp.float32))
+            xs = xbuf[h, :, pl.ds(pl.multiple_of(g * cols, cols), cols)].astype(jnp.float32)
+            ybuf[cb, h] = (xs + branch).astype(jnp.bfloat16)
+            own_out(cb, h).start()
+        start(cb, 4)
+
+    def stage5(cb):
+        finish(cb, 4)
+        start(cb, 5)
+
+    def stage6(cb):
+        finish(cb, 5)
+        for h in range(2):
+            own_out(cb, h).wait()
+        start(cb, 6)
+
+    def stage7(cb):
+        finish(cb, 6)
+        start(cb, 7)
+
+    def stage8(cb):
+        finish(cb, 7)
+
+    stages = (stage0, stage1, stage2, stage3, stage4, stage5, stage6, stage7, stage8)
+
+    @pl.loop(0, COL + len(stages) - 1)
+    def _(n):
+        for s, fn in enumerate(stages):
+            cb = n - s
+
+            @pl.when(jnp.logical_and(cb >= 0, cb < COL))
+            def _(fn=fn, cb=cb):
+                fn(cb)
+
+
+MT = 512
+
+
+def reduce_call(az, x, wo, wd):
+    seq, kk = az.shape
+    d = x.shape[1]
+    cols = d // COL
+    half = seq // 2
+    big, small = half // TPA, half // TPA // TPA
+    bf = jnp.bfloat16
+    hbm = pl.BlockSpec(memory_space=pl.ANY)
+    vm = pl.BlockSpec(memory_space=pltpu.VMEM)
+    res = pl.pallas_call(
+        reduce_kernel,
+        out_shape=jax.ShapeDtypeStruct((COL, seq, cols), bf),
+        in_specs=[vm, hbm, hbm, hbm],
+        out_specs=hbm,
+        scratch_shapes=[
+            pltpu.VMEM((COL, kk, cols), bf),
+            pltpu.VMEM((COL, seq, cols), bf),
+            pltpu.VMEM((COL, 2, 2, big // 2, cols), bf),
+            pltpu.VMEM((COL, 2, 2, big, cols), bf),
+            pltpu.VMEM((COL, 2, 2, small // 2, cols), bf),
+            pltpu.VMEM((COL, 2, 2, small, cols), bf),
+            pltpu.VMEM((COL, 2, small, cols), bf),
+            pltpu.VMEM((2, small, d), bf),
+            pltpu.SemaphoreType.DMA((COL, 2, 2, 8)),
+            pltpu.SemaphoreType.DMA((COL, 2, 2, 8)),
+            pltpu.SemaphoreType.DMA((8,)),
+            pltpu.SemaphoreType.DMA((8,)),
+            pltpu.SemaphoreType.DMA((4,)),
+            pltpu.SemaphoreType.DMA((COL, 2)),
+        ],
+        compiler_params=pltpu.CompilerParams(collective_id=1, has_side_effects=True, vmem_limit_bytes=60 * 1024 * 1024),
+        cost_estimate=pl.CostEstimate(flops=2 * seq * kk * d, bytes_accessed=4 * seq * d, transcendentals=0),
+        name="down_reduce",
+    )(az, x, wo, wd)
+    return res.transpose(1, 0, 2).reshape(1, seq, d)
+
+
 def solution(mesh):
     row_spec = P(("dp", "fsdp"), None, None)
 
     def local_layer(hidden, positions, norm_gain, w_query, w_key, w_value, w_gate, w_up, w_out, w_down):
         gain_full = lax.all_gather(norm_gain, "fsdp", axis=0, tiled=True)
-        wq_full = lax.all_gather(w_query, "fsdp", axis=0, tiled=True)
-        wk_full = lax.all_gather(w_key, "fsdp", axis=0, tiled=True)
-        wv_full = lax.all_gather(w_value, "fsdp", axis=0, tiled=True)
-        wg_full = lax.all_gather(w_gate, "fsdp", axis=0, tiled=True)
-        wu_full = lax.all_gather(w_up, "fsdp", axis=0, tiled=True)
-        wo_full = lax.all_gather(w_out, "fsdp", axis=1, tiled=True)
-        wd_full = lax.all_gather(w_down, "fsdp", axis=1, tiled=True)
+        w_in = jnp.concatenate([w_query, w_key, w_value, w_gate, w_up], axis=1)
+        w_in = lax.all_gather(w_in, "fsdp", axis=0, tiled=True)
         batch = hidden.shape[0]
         seq_len = hidden.shape[1]
-        head_dim = wk_full.shape[1]
+        head_dim = w_key.shape[1]
+        ff = w_gate.shape[1]
         normed = layer_norm(hidden, gain_full)
-        query_raw = project(normed, wq_full).astype(jnp.bfloat16)
-        key_raw = project(normed, wk_full).astype(jnp.bfloat16)
-        values = project(normed, wv_full).astype(jnp.bfloat16)
-        gate_raw = project(normed, wg_full).astype(jnp.bfloat16)
-        up_raw = project(normed, wu_full).astype(jnp.bfloat16)
+        raw = project(normed, w_in).astype(jnp.bfloat16)
+        query_raw, key_raw, values = raw[..., :head_dim], raw[..., head_dim:2 * head_dim], raw[..., 2 * head_dim:3 * head_dim]
+        gate_raw, up_raw = raw[..., 3 * head_dim:3 * head_dim + ff], raw[..., 3 * head_dim + ff:]
         cos_t, sin_t = rope_tables(positions, head_dim)
         query_rot = rope_rotate(query_raw.reshape(batch, seq_len, -1, head_dim).astype(jnp.float32), cos_t[:, None, :], sin_t[:, None, :]).astype(jnp.bfloat16)
         key_rot = rope_rotate(key_raw.astype(jnp.float32), cos_t, sin_t).astype(jnp.bfloat16)
         attn_out = causal_attention(query_rot, key_rot, values)
         gated_act = (jax.nn.silu(gate_raw.astype(jnp.float32)) * up_raw.astype(jnp.float32)).astype(jnp.bfloat16)
-        branch = project(attn_out, wo_full) + project(gated_act, wd_full)
-        branch = lax.psum(branch.astype(jnp.bfloat16), "tp")
-        return (hidden.astype(jnp.float32) + branch.astype(jnp.float32)).astype(jnp.bfloat16)
+        az = jnp.concatenate([attn_out, gated_act], axis=-1)[0]
+        return reduce_call(az, hidden[0], w_out, w_down)
 
     in_specs = (row_spec, P(None), P("fsdp"), P("fsdp", "tp"), P("fsdp", None), P("fsdp", None), P("fsdp", "tp"), P("fsdp", "tp"), P("tp", "fsdp"), P("tp", "fsdp"))
     return jax.shard_map(local_layer, mesh=mesh, in_specs=in_specs, out_specs=row_spec, check_vma=False)

time: 577 us -> 483 us (0.84); the launches traced: 568 us -> 482 us
  waiting for transfers between devices: 347 us -> 79.3 us
  Pallas kernels: 4.53 us -> 205 us
  matrix products: 128 us -> 69.3 us
  local copies, waits for them, and re-layouts: 6.12 us -> 54 us
  other arithmetic: 54.6 us -> 48.3 us
    psum x1 -> x0, waiting for transfers between devices: 221 us -> none  [local_layer(): branch = lax.psum(branch.astype(jnp.bfloat16), 'tp')]
    pallas_call x0 -> x1, Pallas kernels: none -> 205 us  [reduce_call(): pl.pallas_call(reduce_kernel, out_shape=jax.ShapeDtypeStruct((COL, seq, c...]
    dot_general x6 -> x1, matrix products: 121 us -> 59.6 us  [project(): jnp.einsum('bsn,nm->bsm', operand, weight, preferred_element_type=jnp.flo...]
    all_gather x7 -> x1, waiting for transfers between devices: 122 us -> 79.2 us  [local_layer(): w_in = lax.all_gather(w_in, 'fsdp', axis=0, tiled=True)]
    transpose x0 -> x1, local copies, waits for them, and re-layouts: none -> 21.6 us  [reduce_call(): return res.transpose(1, 0, 2).reshape(1, seq, d)]
    reshape x0 -> x1, local copies, waits for them, and re-layouts: none -> 21.2 us  [reduce_call(): return res.transpose(1, 0, 2).reshape(1, seq, d)]
    another operation x1 -> x0, other arithmetic: 10.3 us -> none
    convert_element_type x4 -> x2, other arithmetic: 19.7 us -> 13.9 us  [the longest x1 9.09 us: local_layer(): rope_rotate(key_raw.astype(jnp.float32), cos_t, sin_t).astype(jnp.bfloat16)]
  transfers between devices with their start and end apart: 8 -> 1, of which waited for: 6 -> 1; matrix products, arithmetic and copies ran while one was open for 20% -> 4% of each run, Pallas kernels for 1% -> 0%
where the time goes in v1:
time: 483 us; the launch traced here: 482 us
  Pallas kernels  205 us (42%)
  waiting for transfers between devices  79.3 us (16%)
  matrix products  69.3 us (14%)
  local copies, waits for them, and re-layouts  54 us (11%)
  other arithmetic  48.3 us (10%)
  between operations  13.7 us (3%)
  blocking collectives  12.1 us (3%)
    pallas_call x1, Pallas kernels, reduce_call(): pl.pallas_call(reduce_kernel, out_shape=jax.ShapeDtypeStruct((COL, seq, c...  205 us
    all_gather x1, waiting for transfers between devices, local_layer(): w_in = lax.all_gather(w_in, 'fsdp', axis=0, tiled=True)  79.2 us
    dot_general x1, matrix products, project(): jnp.einsum('bsn,nm->bsm', operand, weight, preferred_element_type=jnp.flo...  59.6 us
    transpose x1, local copies, waits for them, and re-layouts, reduce_call(): return res.transpose(1, 0, 2).reshape(1, seq, d)  21.6 us
    reshape x1, local copies, waits for them, and re-layouts, reduce_call(): return res.transpose(1, 0, 2).reshape(1, seq, d)  21.2 us
    all_gather x1, blocking collectives, local_layer(): gain_full = lax.all_gather(norm_gain, 'fsdp', axis=0, tiled=True)  12.1 us
    unnamed x24, local copies, waits for them, and re-layouts  11.1 us
  transfers between devices with their start and end apart: 1, of which 1 were waited for; matrix products, arithmetic and copies ran while one was open for 4% of the time, Pallas kernels for 0%

profile of v1, /device:TPU:0, one launch (start us, length us, event | category | flops | bytes accessed | tf_op | source)
XLA Modules:
  0.0 481.9 jit_solution(4454368586155250295)
XLA Ops:
  6.5 0.0 all-gather.3.cloned.1.call-start
  6.5 1.1 constant_dynamic-update-slice_fusion.4
  7.6 1.0 constant_dynamic-update-slice_fusion.3
  8.6 1.0 constant_dynamic-update-slice_fusion.2
  9.5 0.0 copy-start.5
  9.6 0.0 copy-start.6
  9.6 1.3 constant_dynamic-update-slice_fusion.1
  10.9 0.0 copy-done.4
  10.9 0.1 constant_dynamic-update-slice_fusion
  11.0 0.0 copy-start.3
  11.0 1.6 copy-done.3
  12.5 0.0 all-gather.3.cloned.1.call-update
  12.6 12.1 %all-gather = f32[8,1,512]{2,1,0:T(1,128)S(1)} all-gather(f32[1,1,512]{2,1,0:T(1,128)S(1)} %bitcast.96), channel_id=1, replica_groups=mesh['dp'=1,'tp'=16,'fsdp'=8] {'fsdp'}, dimensions={0}, use_global_device_ids=true | all-gather | bytes 18432 | tf_op jit(solution)/shard_map/all_gather | solution.py:361
  24.7 0.6 iota_add_fusion.2
  25.3 0.6 iota_add_fusion.1
  25.9 0.6 iota_add_fusion
  26.5 9.2 %convert_reduce_fusion = f32[2048]{0:T(1024)S(1)} fusion(bf16[1,2048,4096]{2,1,0:T(8,128)(2,1)} %param.10), kind=kLoop, calls=%fused_computation.1 | loop fusion | flops 16775168 | bytes 16785408 | tf_op jit(solution)/shard_map/reduce_sum | solution.py:27
  35.7 4.1 copy-done
  39.8 5.8 %fusion.2 = f32[2048]{0:T(1024)S(1)} fusion(bf16[1,2048,4096]{2,1,0:T(8,128)(2,1)S(1)} %copy-done, f32[2048]{0:T(1024)S(1)} %broadcast_multiply_fusion), kind=kLoop, calls=%fused_computation.4 | loop fusion | flops 33552384 | bytes 16793600 | tf_op jit(solution)/shard_map/reduce_sum | solution.py:28
  45.6 1.7 multiply_bitcast_fusion.1
  47.3 79.2 %all-gather.3.cloned.1.call-done = bf16[4096,2816]{1,0:T(8,128)(2,1)} async-done(((bf16[512,2816]{1,0:T(8,128)(2,1)}), bf16[4096,2816]{1,0:T(8,128)(2,1)}) %all-gather.3.cloned.1.call-update) | async-done | bytes 23068688 | tf_op jit(solution)/shard_map/all_gather | solution.py:363
  126.5 59.6 %convert_bitcast_fusion = bf16[1,2048,2816]{2,1,0:T(8,128)(2,1)} fusion(bf16[4096,2816]{1,0:T(8,128)(2,1)} %all-gather.3.cloned.1.call-done, bf16[1,2048,4096]{2,1,0:T(8,128)(2,1)} %param.10, f32[4096]{0:T(1024)S(1)} %bitcast.95, f32[2048]{0:T(1024)S(1)} %add_rsqrt_fusion, f32[2048]{0:T(1024)S(1)} %broadcast_multiply_fusion), kind=kOutput, calls=%fused_computation.12 | convolution fusion | flops 47292350464 | bytes 51412992 | tf_op jit(solution)/shard_map/bsn,nm->bsm/dot_general | solution.py:33
  186.1 1.9 fusion.43
  188.0 4.8 %fusion.17 = bf16[1,2048,1024]{2,1,0:T(8,128)(2,1)S(1)} fusion(bf16[1,2048,2816]{2,1,0:T(8,128)(2,1)} %convert_bitcast_fusion), kind=kLoop, calls=%fused_computation.19 | loop fusion | flops 16777216 | bytes 12582912 | tf_op jit(solution)/shard_map/convert_element_type | solution.py:376
  192.9 0.1 slice_negate_fusion.1
  193.0 0.0 copy-start.2
  193.0 0.1 slice_negate_fusion
  193.2 1.1 copy-done.2
  194.2 8.9 %fusion.25 = bf16[1,2048,1,256]{3,1,2,0:T(8,128)(2,1)S(1)} fusion(f32[1,2048,1,128]{3,1,2,0:T(8,128)S(1)} %copy-done.2, f32[1,2048,1,128]{3,1,2,0:T(8,128)S(1)} %get-tuple-element.8, f32[1,2048,1,128]{3,1,2,0:T(8,128)S(1)} %get-tuple-element.7, bf16[1,2048,2816]{2,1,0:T(8,128)(2,1)} %convert_bitcast_fusion), kind=kLoop, calls=%fused_computation.37 | loop fusion | flops 3670016 | bytes 5242880 | tf_op jit(solution)/shard_map/convert_element_type | solution.py:373
  203.2 9.1 %fusion.31 = bf16[1,2048,256]{2,1,0:T(8,128)(2,1)S(1)} fusion(f32[1,2048,128]{2,1,0:T(8,128)S(1)} %copy-done.1, f32[1,2048,128]{2,1,0:T(8,128)S(1)} %get-tuple-element.10, f32[1,2048,128]{2,1,0:T(8,128)S(1)} %get-tuple-element.9, bf16[1,2048,2816]{2,1,0:T(8,128)(2,1)} %convert_bitcast_fusion), kind=kLoop, calls=%fused_computation.44 | loop fusion | flops 3670016 | bytes 5242880 | tf_op jit(solution)/shard_map/convert_element_type | solution.py:374
  212.3 0.3 fusion.49
  212.6 0.2 fusion.45
  212.8 1.3 fusion.39
  214.1 0.0 copy-done.9
  214.1 0.6 fusion.48
  214.8 0.5 fusion.34
  215.3 1.6 fusion.41
  216.9 0.8 fusion.47
  217.7 0.6 fusion.20
  218.3 1.9 fusion.42
  220.2 1.0 fusion.46
  221.1 0.7 fusion.18
  221.9 2.1 fusion.40
  224.0 0.1 maximum_bitcast_fusion.1
  224.1 2.9 maximum_bitcast_fusion.az
  226.9 205.3 %down_reduce.1 = bf16[8,2048,512]{2,1,0:T(8,128)(2,1)} custom-call(bf16[2048,1280]{1,0:T(8,128)(2,1)} %maximum_bitcast_fusion.az, bf16[2048,4096]{1,0:T(8,128)(2,1)} %bitcast.92, bf16[256,512]{1,0:T(8,128)(2,1)} %wo.1, bf16[1024,512]{1,0:T(8,128)(2,1)} %wd.1), custom_call_target="tpu_custom_call" | custom-call | flops 21474836480 | bytes 33554432 | tf_op jit(solution)/shard_map/down_reduce/pallas_call | solution.py:329
  432.2 21.6 %copy.13 = bf16[2048,8,512]{0,2,1:T(8,128)(2,1)} copy(bf16[2048,8,512]{2,0,1:T(8,128)(2,1)} %bitcast.94) | data formatting | bytes 33554432 | tf_op jit(solution)/shard_map/transpose | solution.py:354
  453.9 21.2 %copy.14 = bf16[1,2048,4096]{2,1,0:T(8,128)(2,1)} copy(bf16[1,2048,4096]{1,2,0:T(8,128)(2,1)} %bitcast.93) | data formatting | bytes 33554432 | tf_op jit(solution)/shard_map/reshape | solution.py:354
  (15 shorter events, 0.0 us)
Async XLA Ops:
  6.5 120.0 %all-gather.3.cloned.1.call-start = ((), (), s32[]{:S(2)}) async-start(), calls=%async_computation | async-start | bytes 25952256 | tf_op jit(solution)/shard_map/all_gather | solution.py:363
  6.5 4.3 copy-start.4
  9.5 3.0 copy-start.5
  9.6 3.0 copy-start.6
  11.0 1.6 copy-start.3
  26.5 13.3 %copy-start = (bf16[1,2048,4096]{2,1,0:T(8,128)(2,1)S(1)}, bf16[1,2048,4096]{2,1,0:T(8,128)(2,1)}, u32[]{:S(2)}) copy-start(bf16[1,2048,4096]{2,1,0:T(8,128)(2,1)} %param.10) | copy-start | bytes 50331652
  193.0 1.2 copy-start.2
  193.2 10.0 %copy-start.1 = (f32[1,2048,128]{2,1,0:T(8,128)S(1)}, f32[1,2048,128]{2,1,0:T(8,128)}, u32[]{:S(2)}) copy-start(f32[1,2048,128]{2,1,0:T(8,128)} %get-tuple-element.12) | copy-start | bytes 3145732
  212.6 1.5 copy-start.9
  215.3 1.6 copy-start.8
  218.3 1.9 copy-start.7
Sparse Core Ops, SparseCore 0:
  12.7 113.7 all-gather.2

commit v2 on v1

--- a/solution.py
+++ b/solution.py
@@ -5,54 +5,7 @@
 from jax.experimental.pallas import tpu as pltpu
 from jax.sharding import PartitionSpec as P
 
-Q_BLOCK = 512
 NORM_EPS = 1e-6
-
-
-def rope_tables(positions, head_dim):
-    inv_freq = 10000.0 ** (-jnp.arange(0, head_dim, 2, dtype=jnp.float32) / head_dim)
-    angles = positions.astype(jnp.float32)[:, None] * inv_freq[None, :]
-    angles = jnp.concatenate([angles, angles], axis=-1)
-    return jnp.cos(angles), jnp.sin(angles)
-
-
-def rope_rotate(vectors, cos_t, sin_t):
-    half_dim = vectors.shape[-1] // 2
-    rotated = jnp.concatenate([-vectors[..., half_dim:], vectors[..., :half_dim]], axis=-1)
-    return vectors * cos_t + rotated * sin_t
-
-
-def layer_norm(hidden, gain_vec):
-    row_f32 = hidden.astype(jnp.float32)
-    centered = row_f32 - jnp.mean(row_f32, axis=-1, keepdims=True)
-    variance = jnp.mean(centered * centered, axis=-1, keepdims=True)
-    return (centered * lax.rsqrt(variance + NORM_EPS) * gain_vec).astype(jnp.bfloat16)
-
-
-def project(operand, weight):
-    return jnp.einsum("bsn,nm->bsm", operand, weight, preferred_element_type=jnp.float32)
-
-
-def causal_attention(query_rot, key_rot, values):
-    batch = query_rot.shape[0]
-    seq_len = query_rot.shape[1]
-    n_heads = query_rot.shape[2]
-    head_dim = query_rot.shape[3]
-    q_block = min(Q_BLOCK, seq_len)
-    score_scale = head_dim ** -0.5
-    pieces = []
-    for blk_idx in range(seq_len // q_block):
-        blk_lo = blk_idx * q_block
-        blk_hi = blk_lo + q_block
-        scores = jnp.einsum("bshe,bte->bsht", query_rot[:, blk_lo:blk_hi], key_rot[:, :blk_hi], preferred_element_type=jnp.float32) * score_scale
-        causal_mask = jnp.arange(blk_hi)[None, :] <= (blk_lo + jnp.arange(q_block))[:, None]
-        scores = jnp.where(causal_mask[None, :, None, :], scores, -1e30)
-        prob_rows = jax.nn.softmax(scores, axis=-1).astype(jnp.bfloat16)
-        pieces.append(jnp.einsum("bsht,bte->bshe", prob_rows, values[:, :blk_hi], preferred_element_type=jnp.float32).astype(jnp.bfloat16))
-    attn_out = jnp.concatenate(pieces, axis=1)
-    return attn_out.reshape(batch, seq_len, n_heads * head_dim)
-
-
 MESH = pl.DeviceIdType.MESH
 TPA = 4
 COL = 8
@@ -71,6 +24,276 @@
     f_r = ((xc + 1) % 4) * 2 + core
     f_l = ((xc + 3) % 4) * 2 + core
     return xc, core, f_p, f_r, f_l
+
+
+QB = 256
+LN_ROWS = 128
+LN_SUB = 64
+GU = 128
+M1 = 512
+
+
+def project_kernel(x_hbm, pos, inv_freq, gain, wq, wk, wv, wg, wu, az, wbuf, h, q, k, v, cos_t, sin_t, gbuf, xb, scores, acc,
+                   ssem, rsem, gss, grs, lsem, gsem, xsem):
+    f = lax.axis_index("fsdp")
+    nf = lax.axis_size("fsdp")
+    xc, core, f_p, f_r, f_l = _fsdp_ids(f)
+    f_o = ((xc + 2) % 4) * 2 + core
+    seq, d = h.shape
+    depth = wq.shape[0]
+    mid = depth // 2
+    hd = wq.shape[1]
+    n_chunk = wbuf.shape[0]
+    n_ff = wg.shape[1] // GU
+
+    def rows_of(dev):
+        return pl.ds(pl.multiple_of(dev * depth, depth), depth)
+
+    def half_of(dev, part):
+        return pl.ds(pl.multiple_of(dev * depth + part * mid, mid), mid)
+
+    def load(i, part, src, col):
+        return pltpu.make_async_copy(src.at[:, pl.ds(col, GU)], wbuf.at[i, rows_of(f), pl.ds(part * GU, GU)], lsem.at[i, part])
+
+    for i, w in enumerate((wq, wk, wv)):
+        for part in range(2):
+            load(i, part, w, part * GU).start()
+    for j in range(n_ff):
+        load(3 + j, 0, wg, j * GU).start()
+        load(3 + j, 1, wu, j * GU).start()
+
+    def load_x(blk):
+        slot = blk % 2
+        return pltpu.make_async_copy(x_hbm.at[pl.ds(pl.multiple_of(blk * LN_ROWS, LN_ROWS), LN_ROWS), :], xb.at[slot], xsem.at[slot])
+
+    load_x(0).start()
+    ld_g = pltpu.make_async_copy(gain, gbuf.at[:, pl.ds(pl.multiple_of(f * depth, depth), depth)], gsem)
+    ld_g.start()
+
+    barrier = pltpu.get_barrier_semaphore()
+    for e in range(1, nf):
+        pl.semaphore_signal(barrier, inc=1, device_id={"fsdp": (f + e) % nf}, device_id_type=MESH)
+    pl.semaphore_wait(barrier, nf - 1)
+
+    def rcopy(i, s, src, dev):
+        return pltpu.make_async_remote_copy(src_ref=src, dst_ref=src, send_sem=ssem.at[i, s], recv_sem=rsem.at[i, s],
+                                            device_id={"fsdp": dev}, device_id_type=MESH)
+
+    def transfer(i, s):
+        src, dev = (
+            (lambda: wbuf.at[i, rows_of(f)], f_r),
+            (lambda: wbuf.at[i, rows_of(f)], f_l),
+            (lambda: wbuf.at[i, rows_of(f)], f_p),
+            (lambda: wbuf.at[i, half_of(f_l, 0)], f_r),
+            (lambda: wbuf.at[i, half_of(f_r, 1)], f_l),
+            (lambda: wbuf.at[i, rows_of(f_l)], f_p),
+            (lambda: wbuf.at[i, rows_of(f_r)], f_p),
+            (lambda: wbuf.at[i, rows_of(f_o)], f_p),
+        )[s]
+        return rcopy(i, s, src(), dev)
+
+    def send_own(i):
+        for part in range(2):
+            load(i, part, wq, part * GU).wait()
+        for s in range(3):
+            transfer(i, s).start()
+
+    def net_a(i):
+        transfer(i, 0).wait_recv()
+        transfer(i, 3).start()
+        transfer(i, 1).wait_recv()
+        transfer(i, 4).start()
+
+        @pl.when(i + 2 < n_chunk)
+        def _():
+            send_own(i + 2)
+
+        transfer(i, 5).start()
+        transfer(i, 6).start()
+
+    def net_b(i):
+        transfer(i, 3).wait_recv()
+        transfer(i, 4).wait_recv()
+        transfer(i, 7).start()
+
+    def ready(i):
+        for s in (2, 5, 6, 7):
+            transfer(i, s).wait_recv()
+        for s in range(8):
+            transfer(i, s).wait_send()
+
+    ld_g.wait()
+    gcol = gbuf.at[:, pl.ds(pl.multiple_of(f * depth, depth), depth)]
+    gcopies = [pltpu.make_async_remote_copy(src_ref=gcol, dst_ref=gcol, send_sem=gss.at[e], recv_sem=grs.at[e],
+                                            device_id={"fsdp": (f + e) % nf}, device_id_type=MESH) for e in range(1, nf)]
+    for c in gcopies:
+        c.start()
+    send_own(0)
+    send_own(1)
+
+    @pl.loop(0, seq // QB)
+    def _(b):
+        rows = pl.ds(pl.multiple_of(b * QB, QB), QB)
+        angle = pos[rows, :].astype(jnp.float32) * inv_freq[...]
+        cos_t[rows, :] = jnp.cos(angle)
+        sin_t[rows, :] = jnp.sin(angle)
+
+    for c in gcopies:
+        c.wait()
+
+    n_blk = seq // LN_ROWS
+
+    def norm_blocks(lo, hi):
+        @pl.loop(lo, hi)
+        def _(blk):
+            load_x(blk).wait()
+
+            @pl.when(blk + 1 < n_blk)
+            def _():
+                load_x(blk + 1).start()
+
+            @pl.loop(0, LN_ROWS // LN_SUB)
+            def _(r):
+                row = xb[blk % 2, pl.ds(pl.multiple_of(r * LN_SUB, LN_SUB), LN_SUB), :].astype(jnp.float32)
+                centered = row - jnp.sum(row, axis=-1, keepdims=True) * (1.0 / d)
+                var = jnp.sum(centered * centered, axis=-1, keepdims=True) * (1.0 / d)
+                out = centered * lax.rsqrt(var + NORM_EPS) * gbuf[...]
+                h[pl.ds(pl.multiple_of(blk * LN_ROWS + r * LN_SUB, LN_SUB), LN_SUB), :] = out.astype(jnp.bfloat16)
+
+    norm_blocks(0, n_blk // 2)
+    net_a(0)
+    norm_blocks(n_blk // 2, n_blk)
+
+    def rope(rows):
+        y = acc[...].astype(jnp.bfloat16).astype(jnp.float32)
+        a, b = y[:, :hd // 2], y[:, hd // 2:]
+        c, s = cos_t[rows, :], sin_t[rows, :]
+        return jnp.concatenate([a * c - b * s, b * c + a * s], axis=1).astype(jnp.bfloat16)
+
+    def compute(i):
+        @pl.loop(0, seq // M1)
+        def _(m):
+            rows = pl.ds(pl.multiple_of(m * M1, M1), M1)
+            acc[...] = jnp.dot(h[rows, :], wbuf[i], preferred_element_type=jnp.float32)
+
+            @pl.when(i == 0)
+            def _():
+                q[rows, :] = rope(rows)
+
+            @pl.when(i == 1)
+            def _():
+                k[rows, :] = rope(rows)
+
+            @pl.when(i == 2)
+            def _():
+                v[rows, :] = acc[...].astype(jnp.bfloat16)
+
+            @pl.when(i >= 3)
+            def _():
+                g = acc[:, :GU].astype(jnp.bfloat16).astype(jnp.float32)
+                u = acc[:, GU:].astype(jnp.bfloat16).astype(jnp.float32)
+                z = (g * (1.0 / (1.0 + jnp.exp(-g)))) * u
+                az[rows, pl.ds(pl.multiple_of(hd + (i - 3) * GU, GU), GU)] = z.astype(jnp.bfloat16)
+
+    scale = hd ** -0.5
+
+    def tile(b):
+        return pl.ds(pl.multiple_of(b * QB, QB), QB)
+
+    def attend(b):
+        qb = q[tile(b), :]
+
+        def score(t):
+            return lax.dot_general(qb, k[tile(t), :], (((1,), (1,)), ((), ())), preferred_element_type=jnp.float32) * scale
+
+        def first(t, m):
+            s = score(t)
+            scores[t] = s
+            return jnp.maximum(m, jnp.max(s, axis=-1, keepdims=True))
+
+        s = score(b)
+        keep = lax.broadcasted_iota(jnp.int32, (QB, QB), 1) <= lax.broadcasted_iota(jnp.int32, (QB, QB), 0)
+        s = jnp.where(keep, s, -1e30)
+        scores[b] = s
+        m = lax.fori_loop(0, b, first, jnp.max(s, axis=-1, keepdims=True))
+
+        def second(t, total):
+            e = jnp.exp(scores[t] - m)
+            scores[t] = e
+            return total + jnp.sum(e, axis=-1, keepdims=True)
+
+        total = lax.fori_loop(0, b + 1, second, jnp.zeros((QB, 1), jnp.float32))
+        inv = 1.0 / total
+        acc[0:QB, :] = jnp.zeros((QB, hd), jnp.float32)
+
+        @pl.loop(0, b + 1)
+        def _(t):
+            p = (scores[t] * inv).astype(jnp.bfloat16)
+            acc[0:QB, :] += jnp.dot(p, v[tile(t), :], preferred_element_type=jnp.float32)
+
+        az[tile(b), 0:hd] = acc[0:QB, :].astype(jnp.bfloat16)
+
+    n_q = seq // QB
+
+    @pl.loop(1, n_chunk + 1)
+    def _(i):
+        @pl.when(i < n_chunk)
+        def _():
+            net_a(i)
+
+        net_b(i - 1)
+
+        @pl.when(i == 4)
+        def _():
+            attend(0)
+
+        @pl.when(jnp.logical_and(i >= 4, i < 4 + n_q - 1))
+        def _():
+            attend(i - 3)
+
+        ready(i - 1)
+        compute(i - 1)
+
+
+def project_call(x, positions, norm_gain, w_query, w_key, w_value, w_gate, w_up):
+    seq, d = x.shape
+    depth, hd = w_query.shape
+    ff = w_gate.shape[1]
+    n_chunk = 3 + ff // GU
+    inv_freq = 10000.0 ** (-jnp.arange(0, hd, 2, dtype=jnp.float32) / hd)
+    bf, f32 = jnp.bfloat16, jnp.float32
+    hbm = pl.BlockSpec(memory_space=pl.ANY)
+    vm = pl.BlockSpec(memory_space=pltpu.VMEM)
+    flops = 2 * seq * d * (3 * hd + 2 * ff) + 2 * seq * seq * hd
+    return pl.pallas_call(
+        project_kernel,
+        out_shape=jax.ShapeDtypeStruct((seq, hd + ff), bf),
+        in_specs=[hbm, vm, vm] + [hbm] * 6,
+        out_specs=vm,
+        scratch_shapes=[
+            pltpu.VMEM((n_chunk, d, hd), bf),
+            pltpu.VMEM((seq, d), bf),
+            pltpu.VMEM((seq, hd), bf),
+            pltpu.VMEM((seq, hd), bf),
+            pltpu.VMEM((seq, hd), bf),
+            pltpu.VMEM((seq, hd // 2), f32),
+            pltpu.VMEM((seq, hd // 2), f32),
+            pltpu.VMEM((1, d), f32),
+            pltpu.VMEM((2, LN_ROWS, d), bf),
+            pltpu.VMEM((seq // QB, QB, QB), f32),
+            pltpu.VMEM((M1, hd), f32),
+            pltpu.SemaphoreType.DMA((n_chunk, 8)),
+            pltpu.SemaphoreType.DMA((n_chunk, 8)),
+            pltpu.SemaphoreType.DMA((8,)),
+            pltpu.SemaphoreType.DMA((8,)),
+            pltpu.SemaphoreType.DMA((n_chunk, 2)),
+            pltpu.SemaphoreType.DMA,
+            pltpu.SemaphoreType.DMA((2,)),
+        ],
+        compiler_params=pltpu.CompilerParams(collective_id=0, has_side_effects=True, vmem_limit_bytes=63 * 1024 * 1024),
+        cost_estimate=pl.CostEstimate(flops=flops, bytes_accessed=2 * seq * d, transcendentals=0),
+        name="gather_project",
+    )(x, positions.reshape(seq, 1), inv_freq.reshape(1, hd // 2), norm_gain.reshape(1, depth), w_query, w_key, w_value, w_gate, w_up)
 
 
 def reduce_kernel(az, x_hbm, wo, wd, out, wbuf, part, r1, r2, r3, r4, ybuf, xbuf,
@@ -351,30 +574,33 @@
         cost_estimate=pl.CostEstimate(flops=2 * seq * kk * d, bytes_accessed=4 * seq * d, transcendentals=0),
         name="down_reduce",
     )(az, x, wo, wd)
-    return res.transpose(1, 0, 2).reshape(1, seq, d)
+    return repack(res)[None]
+
+
+def repack_kernel(src, dst):
+    cols = src.shape[2]
+    for b in range(COL):
+        dst[:, b * cols:(b + 1) * cols] = src[b]
+
+
+def repack(blocks):
+    n, seq, cols = blocks.shape
+    rows = 128
+    return pl.pallas_call(
+        repack_kernel,
+        grid=(seq // rows,),
+        out_shape=jax.ShapeDtypeStruct((seq, n * cols), blocks.dtype),
+        in_specs=[pl.BlockSpec((n, rows, cols), lambda i: (0, i, 0))],
+        out_specs=pl.BlockSpec((rows, n * cols), lambda i: (i, 0)),
+        name="repack",
+    )(blocks)
 
 
 def solution(mesh):
     row_spec = P(("dp", "fsdp"), None, None)
 
     def local_layer(hidden, positions, norm_gain, w_query, w_key, w_value, w_gate, w_up, w_out, w_down):
-        gain_full = lax.all_gather(norm_gain, "fsdp", axis=0, tiled=True)
-        w_in = jnp.concatenate([w_query, w_key, w_value, w_gate, w_up], axis=1)
-        w_in = lax.all_gather(w_in, "fsdp", axis=0, tiled=True)
-        batch = hidden.shape[0]
-        seq_len = hidden.shape[1]
-        head_dim = w_key.shape[1]
-        ff = w_gate.shape[1]
-        normed = layer_norm(hidden, gain_full)
-        raw = project(normed, w_in).astype(jnp.bfloat16)
-        query_raw, key_raw, values = raw[..., :head_dim], raw[..., head_dim:2 * head_dim], raw[..., 2 * head_dim:3 * head_dim]
-        gate_raw, up_raw = raw[..., 3 * head_dim:3 * head_dim + ff], raw[..., 3 * head_dim + ff:]
-        cos_t, sin_t = rope_tables(positions, head_dim)
-        query_rot = rope_rotate(query_raw.reshape(batch, seq_len, -1, head_dim).astype(jnp.float32), cos_t[:, None, :], sin_t[:, None, :]).astype(jnp.bfloat16)
-        key_rot = rope_rotate(key_raw.astype(jnp.float32), cos_t, sin_t).astype(jnp.bfloat16)
-        attn_out = causal_attention(query_rot, key_rot, values)
-        gated_act = (jax.nn.silu(gate_raw.astype(jnp.float32)) * up_raw.astype(jnp.float32)).astype(jnp.bfloat16)
-        az = jnp.concatenate([attn_out, gated_act], axis=-1)[0]
+        az = project_call(hidden[0], positions, norm_gain, w_query, w_key, w_value, w_gate, w_up)
         return reduce_call(az, hidden[0], w_out, w_down)
 
     in_specs = (row_spec, P(None), P("fsdp"), P("fsdp", "tp"), P("fsdp", None), P("fsdp", None), P("fsdp", "tp"), P("fsdp", "tp"), P("tp", "fsdp"), P("tp", "fsdp"))

time: 483 us -> 353 us (0.73)
  Pallas kernels: 205 us -> 349 us
  waiting for transfers between devices: 79.3 us -> 0 us
  matrix products: 69.3 us -> 0 us
  local copies, waits for them, and re-layouts: 54 us -> 2.04 us
  other arithmetic: 48.3 us -> 0.61 us
  between operations: 13.7 us -> 0.02 us
  blocking collectives: 12.1 us -> 0 us
    pallas_call x0 -> x2, Pallas kernels: none -> 142 us  [the longest x1 125 us: project_call(): pl.pallas_call(project_kernel, out_shape=jax.ShapeDtypeStruct((seq, hd +...]
    all_gather x1 -> x0, waiting for transfers between devices: 79.2 us -> none  [local_layer(): w_in = lax.all_gather(w_in, 'fsdp', axis=0, tiled=True)]
    dot_general x9 -> x0, matrix products: 69.3 us -> none  [the longest x1 59.6 us: project(): jnp.einsum('bsn,nm->bsm', operand, weight, preferred_element_type=jnp.flo...]
    convert_element_type x5 -> x0, other arithmetic: 24.7 us -> none  [the longest x1 9.09 us: local_layer(): rope_rotate(key_raw.astype(jnp.float32), cos_t, sin_t).astype(jnp.bfloat16)]
    transpose x1 -> x0, local copies, waits for them, and re-layouts: 21.6 us -> none  [reduce_call(): return res.transpose(1, 0, 2).reshape(1, seq, d)]
    reshape x1, local copies, waits for them, and re-layouts: 21.2 us -> 2.04 us  [project_call(): positions.reshape(seq, 1)]
    reduce_sum x6 -> x0, other arithmetic: 16.9 us -> none  [the longest x1 9.17 us: layer_norm(): centered = row_f32 - jnp.mean(row_f32, axis=-1, keepdims=True)]
    all_gather x1 -> x0, blocking collectives: 12.1 us -> none  [local_layer(): gain_full = lax.all_gather(norm_gain, 'fsdp', axis=0, tiled=True)]
  transfers between devices with their start and end apart: 1 -> 0, of which waited for: 1 -> 0; matrix products, arithmetic and copies ran while one was open for 4% -> 0% of each run, Pallas kernels for 0% -> 0%
where the time goes in v2:
time: 353 us; the launch traced here: 352 us
  Pallas kernels  349 us (99%)
    pallas_call x1, Pallas kernels, reduce_call(): pl.pallas_call(reduce_kernel, out_shape=jax.ShapeDtypeStruct((COL, seq, c...  207 us
    pallas_call x1, Pallas kernels, project_call(): pl.pallas_call(project_kernel, out_shape=jax.ShapeDtypeStruct((seq, hd +...  125 us
    pallas_call x1, Pallas kernels, repack(): pl.pallas_call(repack_kernel, grid=(seq // rows,), out_shape=jax.ShapeDty...  17.4 us

profile of v2, /device:TPU:0, one launch (start us, length us, event | category | flops | bytes accessed | tf_op | source)
XLA Modules:
  0.0 351.9 jit_solution(8150385903638879517)
XLA Ops:
  0.0 0.6 multiply_power_fusion.inv_freq
  0.6 2.0 copy.11.pos
  2.6 124.7 %gather_project.1.az = bf16[2048,1280]{1,0:T(8,128)(2,1)} custom-call(bf16[2048,4096]{1,0:T(8,128)(2,1)} %bitcast.5, s32[2048,1]{1,0:T(8,128)} %copy.11.pos, f32[1,128]{1,0:T(1,128)} %multiply_power_fusion.inv_freq, f32[1,512]{1,0:T(1,128)} %bitcast.7, bf16[512,256]{1,0:T(8,128)(2,1)} %wq.1, bf16[512,256]{1,0:T(8,128)(2,1)} %wk.1, bf16[512,256]{1,0:T(8,128)(2,1)} %wv.1, ...), custom_call_target="tpu_custom_call" | custom-call | flops 49392123904 | bytes 16777216 | tf_op jit(solution)/shard_map/gather_project/pallas_call | solution.py:268
  127.3 207.2 %down_reduce.1.src = bf16[8,2048,512]{2,1,0:T(8,128)(2,1)} custom-call(bf16[2048,1280]{1,0:T(8,128)(2,1)} %gather_project.1.az, bf16[2048,4096]{1,0:T(8,128)(2,1)} %bitcast.6, bf16[256,512]{1,0:T(8,128)(2,1)} %wo.1, bf16[1024,512]{1,0:T(8,128)(2,1)} %wd.1), custom_call_target="tpu_custom_call" | custom-call | flops 21474836480 | bytes 33554432 | tf_op jit(solution)/shard_map/down_reduce/pallas_call | solution.py:552
  334.5 17.4 %repack.1 = bf16[2048,4096]{1,0:T(8,128)(2,1)} custom-call(bf16[8,2048,512]{2,1,0:T(8,128)(2,1)} %down_reduce.1.src), custom_call_target="tpu_custom_call" | custom-call | tf_op jit(solution)/shard_map/repack/pallas_call | solution.py:589

commit v3 on v2

--- a/solution.py
+++ b/solution.py
@@ -1,5 +1,6 @@
 import jax
 import jax.numpy as jnp
+import numpy as np
 from jax import lax
 from jax.experimental import pallas as pl
 from jax.experimental.pallas import tpu as pltpu
@@ -28,9 +29,10 @@
 
 QB = 256
 LN_ROWS = 128
+X_SLOTS = 4
 LN_SUB = 64
 GU = 128
-M1 = 512
+M1 = 1024
 
 
 def project_kernel(x_hbm, pos, inv_freq, gain, wq, wk, wv, wg, wu, az, wbuf, h, q, k, v, cos_t, sin_t, gbuf, xb, scores, acc,
@@ -63,10 +65,11 @@
         load(3 + j, 1, wu, j * GU).start()
 
     def load_x(blk):
-        slot = blk % 2
+        slot = blk % X_SLOTS
         return pltpu.make_async_copy(x_hbm.at[pl.ds(pl.multiple_of(blk * LN_ROWS, LN_ROWS), LN_ROWS), :], xb.at[slot], xsem.at[slot])
 
-    load_x(0).start()
+    for blk in range(X_SLOTS - 1):
+        load_x(blk).start()
     ld_g = pltpu.make_async_copy(gain, gbuf.at[:, pl.ds(pl.multiple_of(f * depth, depth), depth)], gsem)
     ld_g.start()
 
@@ -131,10 +134,15 @@
     send_own(0)
     send_own(1)
 
-    @pl.loop(0, seq // QB)
+    lanes = pos.shape[1]
+    eye = lax.broadcasted_iota(jnp.int32, (lanes, lanes), 0) == lax.broadcasted_iota(jnp.int32, (lanes, lanes), 1)
+
+    @pl.loop(0, seq // lanes)
     def _(b):
-        rows = pl.ds(pl.multiple_of(b * QB, QB), QB)
-        angle = pos[rows, :].astype(jnp.float32) * inv_freq[...]
+        rows = pl.ds(pl.multiple_of(b * lanes, lanes), lanes)
+        line = pos[pl.ds(b, 1), :].astype(jnp.float32)
+        column = jnp.sum(jnp.where(eye, line, 0.0), axis=-1, keepdims=True)
+        angle = column * inv_freq[...]
         cos_t[rows, :] = jnp.cos(angle)
         sin_t[rows, :] = jnp.sin(angle)
 
@@ -148,13 +156,13 @@
         def _(blk):
             load_x(blk).wait()
 
-            @pl.when(blk + 1 < n_blk)
+            @pl.when(blk + X_SLOTS - 1 < n_blk)
             def _():
-                load_x(blk + 1).start()
+                load_x(blk + X_SLOTS - 1).start()
 
             @pl.loop(0, LN_ROWS // LN_SUB)
             def _(r):
-                row = xb[blk % 2, pl.ds(pl.multiple_of(r * LN_SUB, LN_SUB), LN_SUB), :].astype(jnp.float32)
+                row = xb[blk % X_SLOTS, pl.ds(pl.multiple_of(r * LN_SUB, LN_SUB), LN_SUB), :].astype(jnp.float32)
                 centered = row - jnp.sum(row, axis=-1, keepdims=True) * (1.0 / d)
                 var = jnp.sum(centered * centered, axis=-1, keepdims=True) * (1.0 / d)
                 out = centered * lax.rsqrt(var + NORM_EPS) * gbuf[...]
@@ -196,44 +204,31 @@
                 az[rows, pl.ds(pl.multiple_of(hd + (i - 3) * GU, GU), GU)] = z.astype(jnp.bfloat16)
 
     scale = hd ** -0.5
-
-    def tile(b):
-        return pl.ds(pl.multiple_of(b * QB, QB), QB)
+    n_q = seq // QB
 
     def attend(b):
-        qb = q[tile(b), :]
-
-        def score(t):
-            return lax.dot_general(qb, k[tile(t), :], (((1,), (1,)), ((), ())), preferred_element_type=jnp.float32) * scale
-
-        def first(t, m):
-            s = score(t)
-            scores[t] = s
-            return jnp.maximum(m, jnp.max(s, axis=-1, keepdims=True))
-
-        s = score(b)
-        keep = lax.broadcasted_iota(jnp.int32, (QB, QB), 1) <= lax.broadcasted_iota(jnp.int32, (QB, QB), 0)
-        s = jnp.where(keep, s, -1e30)
-        scores[b] = s
-        m = lax.fori_loop(0, b, first, jnp.max(s, axis=-1, keepdims=True))
-
-        def second(t, total):
-            e = jnp.exp(scores[t] - m)
-            scores[t] = e
-            return total + jnp.sum(e, axis=-1, keepdims=True)
-
-        total = lax.fori_loop(0, b + 1, second, jnp.zeros((QB, 1), jnp.float32))
-        inv = 1.0 / total
-        acc[0:QB, :] = jnp.zeros((QB, hd), jnp.float32)
-
-        @pl.loop(0, b + 1)
-        def _(t):
-            p = (scores[t] * inv).astype(jnp.bfloat16)
-            acc[0:QB, :] += jnp.dot(p, v[tile(t), :], preferred_element_type=jnp.float32)
-
-        az[tile(b), 0:hd] = acc[0:QB, :].astype(jnp.bfloat16)
-
-    n_q = seq // QB
+        rows = pl.ds(b * QB, QB)
+        qb = q[rows, :]
+        peak = None
+        for t in range(b + 1):
+            s = lax.dot_general(qb, k[pl.ds(t * QB, QB), :], (((1,), (1,)), ((), ())), preferred_element_type=jnp.float32) * scale
+            if t == b:
+                keep = lax.broadcasted_iota(jnp.int32, (QB, QB), 1) <= lax.broadcasted_iota(jnp.int32, (QB, QB), 0)
+                s = jnp.where(keep, s, -1e30)
+            scores[:, t * QB:(t + 1) * QB] = s
+            s = jnp.maximum(s[:, :128], s[:, 128:])
+            peak = s if peak is None else jnp.maximum(peak, s)
+        peak = jnp.max(peak, axis=-1, keepdims=True)
+        total = None
+        for t in range(b + 1):
+            e = jnp.exp(scores[:, t * QB:(t + 1) * QB] - peak)
+            scores[:, t * QB:(t + 1) * QB] = e
+            e = e[:, :128] + e[:, 128:]
+            total = e if total is None else total + e
+        inv = 1.0 / jnp.sum(total, axis=-1, keepdims=True)
+        p = (scores[:, :(b + 1) * QB] * inv).astype(jnp.bfloat16)
+        out = jnp.dot(p, v[pl.ds(0, (b + 1) * QB), :], preferred_element_type=jnp.float32)
+        az[rows, 0:hd] = out.astype(jnp.bfloat16)
 
     @pl.loop(1, n_chunk + 1)
     def _(i):
@@ -243,13 +238,10 @@
 
         net_b(i - 1)
 
-        @pl.when(i == 4)
-        def _():
-            attend(0)
-
-        @pl.when(jnp.logical_and(i >= 4, i < 4 + n_q - 1))
-        def _():
-            attend(i - 3)
+        for b in range(n_q):
+            @pl.when(i == (3 + b if b else 4))
+            def _(b=b):
+                attend(b)
 
         ready(i - 1)
         compute(i - 1)
@@ -260,7 +252,7 @@
     depth, hd = w_query.shape
     ff = w_gate.shape[1]
     n_chunk = 3 + ff // GU
-    inv_freq = 10000.0 ** (-jnp.arange(0, hd, 2, dtype=jnp.float32) / hd)
+    inv_freq = jnp.asarray((10000.0 ** (-np.arange(0, hd, 2) / hd)).astype(np.float32))
     bf, f32 = jnp.bfloat16, jnp.float32
     hbm = pl.BlockSpec(memory_space=pl.ANY)
     vm = pl.BlockSpec(memory_space=pltpu.VMEM)
@@ -279,8 +271,8 @@
             pltpu.VMEM((seq, hd // 2), f32),
             pltpu.VMEM((seq, hd // 2), f32),
             pltpu.VMEM((1, d), f32),
-            pltpu.VMEM((2, LN_ROWS, d), bf),
-            pltpu.VMEM((seq // QB, QB, QB), f32),
+            pltpu.VMEM((X_SLOTS, LN_ROWS, d), bf),
+            pltpu.VMEM((QB, seq), f32),
             pltpu.VMEM((M1, hd), f32),
             pltpu.SemaphoreType.DMA((n_chunk, 8)),
             pltpu.SemaphoreType.DMA((n_chunk, 8)),
@@ -288,16 +280,16 @@
             pltpu.SemaphoreType.DMA((8,)),
             pltpu.SemaphoreType.DMA((n_chunk, 2)),
             pltpu.SemaphoreType.DMA,
-            pltpu.SemaphoreType.DMA((2,)),
+            pltpu.SemaphoreType.DMA((X_SLOTS,)),
         ],
         compiler_params=pltpu.CompilerParams(collective_id=0, has_side_effects=True, vmem_limit_bytes=63 * 1024 * 1024),
         cost_estimate=pl.CostEstimate(flops=flops, bytes_accessed=2 * seq * d, transcendentals=0),
         name="gather_project",
-    )(x, positions.reshape(seq, 1), inv_freq.reshape(1, hd // 2), norm_gain.reshape(1, depth), w_query, w_key, w_value, w_gate, w_up)
-
-
-def reduce_kernel(az, x_hbm, wo, wd, out, wbuf, part, r1, r2, r3, r4, ybuf, xbuf,
-                  ssem, rsem, wss, wrs, lsem, osem):
+    )(x, positions.reshape(seq // 128, 128), inv_freq.reshape(1, hd // 2), norm_gain.reshape(1, depth), w_query, w_key, w_value, w_gate, w_up)
+
+
+def reduce_kernel(az, x_hbm, wo, wd, out, wbuf, part, r1, r2, r3, r4, xbuf,
+                  ssem, rsem, wss, wrs, lsem):
     t = lax.axis_index("tp")
     f = lax.axis_index("fsdp")
     ring_y, ring_z = _ring_ids(t)
@@ -367,15 +359,15 @@
         o = (i + 2) % TPA
         m = n // 2
         s = pl.multiple_of(base + o * n, m)
-        return (ring_copy(cb, h, 0, step, part.at[cb, pl.ds(s, m)], land.at[cb, h, 0], r),
-                ring_copy(cb, h, 1, step, part.at[cb, pl.ds(s + m, m)], land.at[cb, h, 1], l))
+        return (ring_copy(cb, h, 0, step, part.at[cb % PART_SLOTS, pl.ds(s, m)], land.at[cb % land.shape[0], h, 0], r),
+                ring_copy(cb, h, 1, step, part.at[cb % PART_SLOTS, pl.ds(s + m, m)], land.at[cb % land.shape[0], h, 1], l))
 
     def rs_second(cb, h, step, ring, base, n, land):
         i, r, l = ring
         s_r = pl.multiple_of(base + ((i + 1) % TPA) * n, n)
         s_l = pl.multiple_of(base + ((i + 3) % TPA) * n, n)
-        return (ring_copy(cb, h, 0, step, part.at[cb, pl.ds(s_r, n)], land.at[cb, h, 0], r),
-                ring_copy(cb, h, 1, step, part.at[cb, pl.ds(s_l, n)], land.at[cb, h, 1], l))
+        return (ring_copy(cb, h, 0, step, part.at[cb % PART_SLOTS, pl.ds(s_r, n)], land.at[cb % land.shape[0], h, 0], r),
+                ring_copy(cb, h, 1, step, part.at[cb % PART_SLOTS, pl.ds(s_l, n)], land.at[cb % land.shape[0], h, 1], l))
 
     def rs_update(cb, h, ring, base, n, land):
         i, _, _ = ring
@@ -384,7 +376,7 @@
         s_l = pl.multiple_of(base + ((i + 3) % TPA) * n + m, m)
         for s, d in ((s_r, 0), (s_l, 1)):
             rows = pl.ds(s, m)
-            part[cb, rows] = (part[cb, rows].astype(jnp.float32) + land[cb, h, d].astype(jnp.float32)).astype(jnp.bfloat16)
+            part[cb % PART_SLOTS, rows] = (part[cb % PART_SLOTS, rows].astype(jnp.float32) + land[cb % land.shape[0], h, d].astype(jnp.float32)).astype(jnp.bfloat16)
 
     def ag_first(cb, h, step, ring, src, base, n):
         i, r, l = ring
@@ -417,7 +409,7 @@
             elif step == 3:
                 res.extend(rs_second(cb, h, step, ring2, base2, small, r4))
             elif step == 4:
-                res.extend(ag_first(cb, h, step, ring2, ybuf.at[cb, h], base2, small))
+                res.extend(ag_first(cb, h, step, ring2, None, base2, small))
             elif step == 5:
                 res.extend(ag_second(cb, h, step, ring2, base2, small))
             elif step == 6:
@@ -435,9 +427,6 @@
             c.wait_recv()
             c.wait_send()
 
-    def own_out(cb, h):
-        return pltpu.make_async_copy(ybuf.at[cb, h], out.at[block_of(cb), pl.ds(own_rows(h), small)], osem.at[cb, h])
-
     def stage0(cb):
         @pl.when(cb == 1)
         def _():
@@ -473,7 +462,7 @@
         @pl.loop(0, seq // MT)
         def _(i):
             rows = pl.ds(pl.multiple_of(i * MT, MT), MT)
-            part[cb, rows] = jnp.dot(az[rows, :], wbuf[cb], preferred_element_type=jnp.float32).astype(jnp.bfloat16)
+            part[cb % PART_SLOTS, rows] = jnp.dot(az[rows, :], wbuf[cb], preferred_element_type=jnp.float32).astype(jnp.bfloat16)
 
         start(cb, 0)
 
@@ -487,8 +476,8 @@
         finish(cb, 1)
         for h in range(2):
             rows = pl.ds(pl.multiple_of(h * half + axes[h][0][0] * big, big), big)
-            part[cb, rows] = (part[cb, rows].astype(jnp.float32) + r2[cb, h, 0].astype(jnp.float32)
-                              + r2[cb, h, 1].astype(jnp.float32)).astype(jnp.bfloat16)
+            part[cb % PART_SLOTS, rows] = (part[cb % PART_SLOTS, rows].astype(jnp.float32) + r2[cb % r2.shape[0], h, 0].astype(jnp.float32)
+                              + r2[cb % r2.shape[0], h, 1].astype(jnp.float32)).astype(jnp.bfloat16)
         start(cb, 2)
 
     def stage3(cb):
@@ -501,11 +490,10 @@
         finish(cb, 3)
         g = block_of(cb)
         for h in range(2):
-            branch = (part[cb, pl.ds(own_rows(h), small)].astype(jnp.float32) + r4[cb, h, 0].astype(jnp.float32)
-                      + r4[cb, h, 1].astype(jnp.float32))
+            branch = (part[cb % PART_SLOTS, pl.ds(own_rows(h), small)].astype(jnp.float32) + r4[cb % r4.shape[0], h, 0].astype(jnp.float32)
+                      + r4[cb % r4.shape[0], h, 1].astype(jnp.float32))
             xs = xbuf[h, :, pl.ds(pl.multiple_of(g * cols, cols), cols)].astype(jnp.float32)
-            ybuf[cb, h] = (xs + branch).astype(jnp.bfloat16)
-            own_out(cb, h).start()
+            out[g, pl.ds(own_rows(h), small), :] = (xs + branch).astype(jnp.bfloat16)
         start(cb, 4)
 
     def stage5(cb):
@@ -514,8 +502,6 @@
 
     def stage6(cb):
         finish(cb, 5)
-        for h in range(2):
-            own_out(cb, h).wait()
         start(cb, 6)
 
     def stage7(cb):
@@ -527,17 +513,20 @@
 
     stages = (stage0, stage1, stage2, stage3, stage4, stage5, stage6, stage7, stage8)
 
-    @pl.loop(0, COL + len(stages) - 1)
+    @pl.loop(0, COL + GAP + len(stages) - 1)
     def _(n):
         for s, fn in enumerate(stages):
-            cb = n - s
-
-            @pl.when(jnp.logical_and(cb >= 0, cb < COL))
-            def _(fn=fn, cb=cb):
-                fn(cb)
+            turn = n - s
+
+            @pl.when(jnp.logical_or(jnp.logical_and(turn >= 0, turn < 2), jnp.logical_and(turn >= 2 + GAP, turn < COL + GAP)))
+            def _(fn=fn, turn=turn):
+                fn(jnp.where(turn >= 2, turn - GAP, turn))
 
 
 MT = 512
+PART_SLOTS = 5
+LAND_SLOTS = 4
+GAP = 3
 
 
 def reduce_call(az, x, wo, wd):
@@ -551,48 +540,49 @@
     vm = pl.BlockSpec(memory_space=pltpu.VMEM)
     res = pl.pallas_call(
         reduce_kernel,
-        out_shape=jax.ShapeDtypeStruct((COL, seq, cols), bf),
+        out_shape=pltpu.VMEM((COL, seq, cols), bf),
         in_specs=[vm, hbm, hbm, hbm],
-        out_specs=hbm,
+        out_specs=vm,
         scratch_shapes=[
             pltpu.VMEM((COL, kk, cols), bf),
-            pltpu.VMEM((COL, seq, cols), bf),
+            pltpu.VMEM((PART_SLOTS, seq, cols), bf),
             pltpu.VMEM((COL, 2, 2, big // 2, cols), bf),
-            pltpu.VMEM((COL, 2, 2, big, cols), bf),
+            pltpu.VMEM((LAND_SLOTS, 2, 2, big, cols), bf),
             pltpu.VMEM((COL, 2, 2, small // 2, cols), bf),
             pltpu.VMEM((COL, 2, 2, small, cols), bf),
-            pltpu.VMEM((COL, 2, small, cols), bf),
             pltpu.VMEM((2, small, d), bf),
             pltpu.SemaphoreType.DMA((COL, 2, 2, 8)),
             pltpu.SemaphoreType.DMA((COL, 2, 2, 8)),
             pltpu.SemaphoreType.DMA((8,)),
             pltpu.SemaphoreType.DMA((8,)),
             pltpu.SemaphoreType.DMA((4,)),
-            pltpu.SemaphoreType.DMA((COL, 2)),
         ],
-        compiler_params=pltpu.CompilerParams(collective_id=1, has_side_effects=True, vmem_limit_bytes=60 * 1024 * 1024),
+        compiler_params=pltpu.CompilerParams(collective_id=1, has_side_effects=True, vmem_limit_bytes=40 * 1024 * 1024),
         cost_estimate=pl.CostEstimate(flops=2 * seq * kk * d, bytes_accessed=4 * seq * d, transcendentals=0),
         name="down_reduce",
     )(az, x, wo, wd)
-    return repack(res)[None]
-
-
-def repack_kernel(src, dst):
-    cols = src.shape[2]
-    for b in range(COL):
-        dst[:, b * cols:(b + 1) * cols] = src[b]
-
-
-def repack(blocks):
+    return write_out(res)[None]
+
+
+def write_kernel(src, dst, sem):
+    n, seq, cols = src.shape
+    copies = [pltpu.make_async_copy(src.at[b], dst.at[:, pl.ds(b * cols, cols)], sem.at[b]) for b in range(n)]
+    for c in copies:
+        c.start()
+    for c in copies:
+        c.wait()
+
+
+def write_out(blocks):
     n, seq, cols = blocks.shape
-    rows = 128
     return pl.pallas_call(
-        repack_kernel,
-        grid=(seq // rows,),
+        write_kernel,
         out_shape=jax.ShapeDtypeStruct((seq, n * cols), blocks.dtype),
-        in_specs=[pl.BlockSpec((n, rows, cols), lambda i: (0, i, 0))],
-        out_specs=pl.BlockSpec((rows, n * cols), lambda i: (i, 0)),
-        name="repack",
+        in_specs=[pl.BlockSpec(memory_space=pltpu.VMEM)],
+        out_specs=pl.BlockSpec(memory_space=pl.ANY),
+        scratch_shapes=[pltpu.SemaphoreType.DMA((n,))],
+        compiler_params=pltpu.CompilerParams(vmem_limit_bytes=24 * 1024 * 1024),
+        name="write_out",
     )(blocks)
 
 

time: 353 us -> 316 us (0.90)
  Pallas kernels: 349 us -> 315 us
    pallas_call x2, Pallas kernels: 225 us -> 201 us  [the longest x1 195 us: reduce_call(): pl.pallas_call(reduce_kernel, out_shape=pltpu.VMEM((COL, seq, cols), bf),...]
    pallas_call x1, Pallas kernels: 125 us -> 115 us  [project_call(): pl.pallas_call(project_kernel, out_shape=jax.ShapeDtypeStruct((seq, hd +...]
where the time goes in v3:
time: 316 us
  Pallas kernels  315 us (100%)
    pallas_call x1, Pallas kernels, reduce_call(): pl.pallas_call(reduce_kernel, out_shape=pltpu.VMEM((COL, seq, cols), bf),...  195 us
    pallas_call x1, Pallas kernels, project_call(): pl.pallas_call(project_kernel, out_shape=jax.ShapeDtypeStruct((seq, hd +...  115 us

profile of v3, /device:TPU:0, one launch (start us, length us, event | category | flops | bytes accessed | tf_op | source)
XLA Modules:
  0.0 315.5 jit_solution(2565615277303696069)
XLA Ops:
  0.0 114.6 %gather_project.1.az = bf16[2048,1280]{1,0:T(8,128)(2,1)} custom-call(bf16[2048,4096]{1,0:T(8,128)(2,1)} %bitcast.4, s32[16,128]{1,0:T(8,128)} %bitcast.6, f32[1,128]{1,0:T(1,128)} %constant.4.inv_freq, f32[1,512]{1,0:T(1,128)} %bitcast.7, bf16[512,256]{1,0:T(8,128)(2,1)} %wq.1, bf16[512,256]{1,0:T(8,128)(2,1)} %wk.1, bf16[512,256]{1,0:T(8,128)(2,1)} %wv.1, ...), custom_call_target="tpu_custom_call" | custom-call | flops 49392123904 | bytes 16777216 | tf_op jit(solution)/shard_map/gather_project/pallas_call | solution.py:260
  114.7 194.9 %down_reduce.1.src = bf16[8,2048,512]{2,1,0:T(8,128)(2,1)S(1)} custom-call(bf16[2048,1280]{1,0:T(8,128)(2,1)} %gather_project.1.az, bf16[2048,4096]{1,0:T(8,128)(2,1)} %bitcast.5, bf16[256,512]{1,0:T(8,128)(2,1)} %wo.1, bf16[1024,512]{1,0:T(8,128)(2,1)} %wd.1), custom_call_target="tpu_custom_call" | custom-call | flops 21474836480 | bytes 33554432 | tf_op jit(solution)/shard_map/down_reduce/pallas_call | solution.py:541
  309.6 5.9 %write_out.1 = bf16[2048,4096]{1,0:T(8,128)(2,1)} custom-call(bf16[8,2048,512]{2,1,0:T(8,128)(2,1)S(1)} %down_reduce.1.src), custom_call_target="tpu_custom_call" | custom-call | tf_op jit(solution)/shard_map/write_out/pallas_call | solution.py:578

commit v4 on v3

--- a/solution.py
+++ b/solution.py
@@ -33,33 +33,37 @@
 LN_SUB = 64
 GU = 128
 M1 = 1024
-
-
-def project_kernel(x_hbm, pos, inv_freq, gain, wq, wk, wv, wg, wu, az, wbuf, h, q, k, v, cos_t, sin_t, gbuf, xb, scores, acc,
-                   ssem, rsem, gss, grs, lsem, gsem, xsem):
+PRE_DOWN = 512
+
+
+def project_kernel(x_hbm, pos, inv_freq, gain, wq, wk, wv, wg, wu, wo, wd, az, pre, wbuf, h, q, k, v, cos_t, sin_t, gbuf, xb, scores, acc,
+                   ssem, rsem, gss, grs, lsem, gsem, xsem, kss, krs, pss, prs):
     f = lax.axis_index("fsdp")
     nf = lax.axis_size("fsdp")
+    t = lax.axis_index("tp")
+    nt = lax.axis_size("tp")
+    ring_y, ring_z = _ring_ids(t)
+    z_id, y_id = ring_z[0], ring_y[0]
     xc, core, f_p, f_r, f_l = _fsdp_ids(f)
     f_o = ((xc + 2) % 4) * 2 + core
     seq, d = h.shape
-    depth = wq.shape[0]
-    mid = depth // 2
-    hd = wq.shape[1]
+    depth = gain.shape[1]
+    hd = wq.shape[3]
     n_chunk = wbuf.shape[0]
-    n_ff = wg.shape[1] // GU
-
-    def rows_of(dev):
-        return pl.ds(pl.multiple_of(dev * depth, depth), depth)
-
-    def half_of(dev, part):
-        return pl.ds(pl.multiple_of(dev * depth + part * mid, mid), mid)
+    n_ff = wg.shape[3] // GU
+    n_x = n_ff + 1
+
+    def half_of(i, dev, part):
+        return wbuf.at[i, dev, pl.ds(part * (TPA // 2), TPA // 2)]
 
     def load(i, part, src, col):
-        return pltpu.make_async_copy(src.at[:, pl.ds(col, GU)], wbuf.at[i, rows_of(f), pl.ds(part * GU, GU)], lsem.at[i, part])
-
-    for i, w in enumerate((wq, wk, wv)):
-        for part in range(2):
-            load(i, part, w, part * GU).start()
+        return pltpu.make_async_copy(src.at[:, :, :, pl.ds(col, GU)], wbuf.at[i, f, :, :, :, pl.ds(part * GU, GU)], lsem.at[i, part])
+
+    ld_kv = [pltpu.make_async_copy(w.at[z_id, y_id], wbuf.at[1 + i, f, z_id, y_id], lsem.at[1 + i, 0]) for i, w in enumerate((wk, wv))]
+    for c in ld_kv:
+        c.start()
+    for part in range(2):
+        load(0, part, wq, part * GU).start()
     for j in range(n_ff):
         load(3 + j, 0, wg, j * GU).start()
         load(3 + j, 1, wu, j * GU).start()
@@ -76,7 +80,9 @@
     barrier = pltpu.get_barrier_semaphore()
     for e in range(1, nf):
         pl.semaphore_signal(barrier, inc=1, device_id={"fsdp": (f + e) % nf}, device_id_type=MESH)
-    pl.semaphore_wait(barrier, nf - 1)
+    for other in (ring_y[1], ring_y[2], ring_z[1], ring_z[2]):
+        pl.semaphore_signal(barrier, inc=1, device_id={"tp": other}, device_id_type=MESH)
+    pl.semaphore_wait(barrier, nf - 1 + 4)
 
     def rcopy(i, s, src, dev):
         return pltpu.make_async_remote_copy(src_ref=src, dst_ref=src, send_sem=ssem.at[i, s], recv_sem=rsem.at[i, s],
@@ -84,16 +90,63 @@
 
     def transfer(i, s):
         src, dev = (
-            (lambda: wbuf.at[i, rows_of(f)], f_r),
-            (lambda: wbuf.at[i, rows_of(f)], f_l),
-            (lambda: wbuf.at[i, rows_of(f)], f_p),
-            (lambda: wbuf.at[i, half_of(f_l, 0)], f_r),
-            (lambda: wbuf.at[i, half_of(f_r, 1)], f_l),
-            (lambda: wbuf.at[i, rows_of(f_l)], f_p),
-            (lambda: wbuf.at[i, rows_of(f_r)], f_p),
-            (lambda: wbuf.at[i, rows_of(f_o)], f_p),
+            (lambda: wbuf.at[i, f], f_r),
+            (lambda: wbuf.at[i, f], f_l),
+            (lambda: wbuf.at[i, f], f_p),
+            (lambda: half_of(i, f_l, 0), f_r),
+            (lambda: half_of(i, f_r, 1), f_l),
+            (lambda: wbuf.at[i, f_l], f_p),
+            (lambda: wbuf.at[i, f_r], f_p),
+            (lambda: wbuf.at[i, f_o], f_p),
         )[s]
         return rcopy(i, s, src(), dev)
+
+    def chunk_of(xi):
+        return xi + 2 * ((xi + n_x - 1) // n_x)
+
+    kv_rings = ((ring_y, ring_z), (ring_z, ring_y))
+
+    def kv_unit(i, dev, lo, n):
+        z, y = (z_id, dev) if i == 0 else (dev, y_id)
+        return wbuf.at[1 + i, pl.ds(lo, n), z, y]
+
+    def kv_line(i, dev, lo, n):
+        return wbuf.at[1 + i, pl.ds(lo, n), dev] if i == 0 else wbuf.at[1 + i, pl.ds(lo, n), :, dev]
+
+    def kv_copies(step):
+        res = []
+        for i in range(2):
+            ids = kv_rings[i][step // 2]
+            me, r, l = ids
+            view = kv_line if step >= 2 else kv_unit
+            if step % 2 == 0:
+                src = (view(i, me, 0, nf), view(i, me, 0, nf))
+            else:
+                src = (view(i, (me + TPA - 1) % TPA, 0, nf // 2), view(i, (me + 1) % TPA, nf // 2, nf // 2))
+            for d_, (part, dev) in enumerate(zip(src, (r, l))):
+                res.append(pltpu.make_async_remote_copy(src_ref=part, dst_ref=part, send_sem=kss.at[nf + step, 2 * i + d_], recv_sem=krs.at[nf + step, 2 * i + d_],
+                                                        device_id={"tp": dev}, device_id_type=MESH))
+        return res
+
+    def kv_start(step):
+        for c in kv_copies(step):
+            c.start()
+
+    def kv_finish(step):
+        for c in kv_copies(step):
+            c.wait_recv()
+            c.wait_send()
+
+    n_o = wo.shape[0]
+    n_d = pre.shape[1] - n_o
+
+    def pre_copies():
+        res = []
+        for d_, dev in ((0, f_r), (1, f_l)):
+            for e, (src, lo, n) in enumerate(((wo, 0, n_o), (wd, n_o, n_d))):
+                res.append(pltpu.make_async_remote_copy(src_ref=src.at[pl.ds(0, n)], dst_ref=pre.at[d_, pl.ds(lo, n)], send_sem=pss.at[d_, e], recv_sem=prs.at[d_, e],
+                                                        device_id={"fsdp": dev}, device_id_type=MESH))
+        return res
 
     def send_own(i):
         for part in range(2):
@@ -101,20 +154,27 @@
         for s in range(3):
             transfer(i, s).start()
 
-    def net_a(i):
+    def net_a(xi):
+        i = chunk_of(xi)
         transfer(i, 0).wait_recv()
         transfer(i, 3).start()
         transfer(i, 1).wait_recv()
         transfer(i, 4).start()
 
-        @pl.when(i + 2 < n_chunk)
-        def _():
-            send_own(i + 2)
+        @pl.when(xi + 2 < n_x)
+        def _():
+            send_own(chunk_of(xi + 2))
+
+        @pl.when(xi + 1 == n_x)
+        def _():
+            for c in pre_copies():
+                c.start()
 
         transfer(i, 5).start()
         transfer(i, 6).start()
 
-    def net_b(i):
+    def net_b(xi):
+        i = chunk_of(xi)
         transfer(i, 3).wait_recv()
         transfer(i, 4).wait_recv()
         transfer(i, 7).start()
@@ -131,8 +191,17 @@
                                             device_id={"fsdp": (f + e) % nf}, device_id_type=MESH) for e in range(1, nf)]
     for c in gcopies:
         c.start()
+    kv_x = []
+    for i in range(2):
+        ld_kv[i].wait()
+        for e in range(1, nf):
+            part = wbuf.at[1 + i, f, z_id, y_id]
+            kv_x.append(pltpu.make_async_remote_copy(src_ref=part, dst_ref=part, send_sem=kss.at[e, i], recv_sem=krs.at[e, i],
+                                                     device_id={"fsdp": (f + e) % nf}, device_id_type=MESH))
+    for c in kv_x:
+        c.start()
     send_own(0)
-    send_own(1)
+    send_own(3)
 
     lanes = pos.shape[1]
     eye = lax.broadcasted_iota(jnp.int32, (lanes, lanes), 0) == lax.broadcasted_iota(jnp.int32, (lanes, lanes), 1)
@@ -148,6 +217,9 @@
 
     for c in gcopies:
         c.wait()
+    for c in kv_x:
+        c.wait()
+    kv_start(0)
 
     n_blk = seq // LN_ROWS
 
@@ -170,7 +242,11 @@
 
     norm_blocks(0, n_blk // 2)
     net_a(0)
+    kv_finish(0)
+    kv_start(1)
     norm_blocks(n_blk // 2, n_blk)
+    kv_finish(1)
+    kv_start(2)
 
     def rope(rows):
         y = acc[...].astype(jnp.bfloat16).astype(jnp.float32)
@@ -182,7 +258,7 @@
         @pl.loop(0, seq // M1)
         def _(m):
             rows = pl.ds(pl.multiple_of(m * M1, M1), M1)
-            acc[...] = jnp.dot(h[rows, :], wbuf[i], preferred_element_type=jnp.float32)
+            acc[...] = jnp.dot(h[rows, :], wbuf[i].reshape(d, hd), preferred_element_type=jnp.float32)
 
             @pl.when(i == 0)
             def _():
@@ -230,24 +306,48 @@
         out = jnp.dot(p, v[pl.ds(0, (b + 1) * QB), :], preferred_element_type=jnp.float32)
         az[rows, 0:hd] = out.astype(jnp.bfloat16)
 
-    @pl.loop(1, n_chunk + 1)
-    def _(i):
-        @pl.when(i < n_chunk)
-        def _():
-            net_a(i)
-
-        net_b(i - 1)
-
-        for b in range(n_q):
-            @pl.when(i == (3 + b if b else 4))
-            def _(b=b):
-                attend(b)
-
-        ready(i - 1)
-        compute(i - 1)
-
-
-def project_call(x, positions, norm_gain, w_query, w_key, w_value, w_gate, w_up):
+    n_first = 3
+
+    @pl.loop(0, n_chunk)
+    def _(j):
+        on_k, on_v = j == n_first + 1, j == n_first + 3
+        xi = j - (j + n_chunk - n_first - 1) // n_chunk - (j + n_chunk - n_first - 3) // n_chunk
+        on_x = jnp.logical_not(jnp.logical_or(on_k, on_v))
+
+        @pl.when(on_x)
+        def _():
+            @pl.when(xi + 1 < n_x)
+            def _():
+                net_a(xi + 1)
+
+            net_b(xi)
+
+        @pl.when(j == 2)
+        def _():
+            kv_finish(2)
+            kv_start(3)
+
+        @pl.when(on_k)
+        def _():
+            kv_finish(3)
+
+        for lo, hi, step in ((0, 4, n_first + 4), (4, 6, n_first + 5), (6, 8, n_first + 6)):
+            @pl.when(j == step)
+            def _(lo=lo, hi=hi):
+                for b in range(lo, hi):
+                    attend(b)
+
+        @pl.when(on_x)
+        def _():
+            ready(chunk_of(xi))
+
+        compute(jnp.where(on_k, 1, jnp.where(on_v, 2, chunk_of(xi))))
+
+    for c in pre_copies():
+        c.wait()
+
+
+def project_call(x, positions, norm_gain, w_query, w_key, w_value, w_gate, w_up, w_out, w_down):
     seq, d = x.shape
     depth, hd = w_query.shape
     ff = w_gate.shape[1]
@@ -259,11 +359,11 @@
     flops = 2 * seq * d * (3 * hd + 2 * ff) + 2 * seq * seq * hd
     return pl.pallas_call(
         project_kernel,
-        out_shape=jax.ShapeDtypeStruct((seq, hd + ff), bf),
-        in_specs=[hbm, vm, vm] + [hbm] * 6,
-        out_specs=vm,
+        out_shape=(jax.ShapeDtypeStruct((seq, hd + ff), bf), jax.ShapeDtypeStruct((2, hd + PRE_DOWN, w_out.shape[1]), bf)),
+        in_specs=[hbm, vm, vm] + [hbm] * 8,
+        out_specs=(vm, hbm),
         scratch_shapes=[
-            pltpu.VMEM((n_chunk, d, hd), bf),
+            pltpu.VMEM((n_chunk, d // depth, TPA, TPA, depth // TPA // TPA, hd), bf),
             pltpu.VMEM((seq, d), bf),
             pltpu.VMEM((seq, hd), bf),
             pltpu.VMEM((seq, hd), bf),
@@ -281,14 +381,19 @@
             pltpu.SemaphoreType.DMA((n_chunk, 2)),
             pltpu.SemaphoreType.DMA,
             pltpu.SemaphoreType.DMA((X_SLOTS,)),
+            pltpu.SemaphoreType.DMA((12, 4)),
+            pltpu.SemaphoreType.DMA((12, 4)),
+            pltpu.SemaphoreType.DMA((2, 2)),
+            pltpu.SemaphoreType.DMA((2, 2)),
         ],
         compiler_params=pltpu.CompilerParams(collective_id=0, has_side_effects=True, vmem_limit_bytes=63 * 1024 * 1024),
         cost_estimate=pl.CostEstimate(flops=flops, bytes_accessed=2 * seq * d, transcendentals=0),
         name="gather_project",
-    )(x, positions.reshape(seq // 128, 128), inv_freq.reshape(1, hd // 2), norm_gain.reshape(1, depth), w_query, w_key, w_value, w_gate, w_up)
-
-
-def reduce_kernel(az, x_hbm, wo, wd, out, wbuf, part, r1, r2, r3, r4, xbuf,
+    )(x, positions.reshape(seq // 128, 128), inv_freq.reshape(1, hd // 2), norm_gain.reshape(1, depth),
+      *(w.reshape(TPA, TPA, depth // TPA // TPA, w.shape[1]) for w in (w_query, w_key, w_value, w_gate, w_up)), w_out, w_down)
+
+
+def reduce_kernel(az, pre, x_hbm, wo, wd, out, wbuf, part, r1, r2, r3, r4, xbuf,
                   ssem, rsem, wss, wrs, lsem):
     t = lax.axis_index("tp")
     f = lax.axis_index("fsdp")
@@ -303,8 +408,13 @@
 
     ld_o = pltpu.make_async_copy(wo, wbuf.at[0, pl.ds(0, hd)], lsem.at[0])
     ld_d = pltpu.make_async_copy(wd, wbuf.at[0, pl.ds(hd, wd.shape[0])], lsem.at[1])
+    n_pre = pre.shape[1]
+    n_rest = wbuf.shape[1] - n_pre
+    ld_pre = [pltpu.make_async_copy(pre.at[e], wbuf.at[2 + 2 * e, pl.ds(0, n_pre)], lsem.at[4 + e]) for e in range(2)]
     ld_o.start()
     ld_d.start()
+    for c in ld_pre:
+        c.start()
     axes = ((ring_y, ring_z), (ring_z, ring_y))
 
     def own_rows(h):
@@ -330,8 +440,9 @@
     kh = kk // 2
     top, bot = pl.ds(0, kh), pl.ds(kh, kh)
     w_own_p = wcopy(0, wbuf.at[0], wbuf.at[1], f_p)
-    w_own_r = wcopy(1, wbuf.at[0], wbuf.at[2], f_r)
-    w_own_l = wcopy(2, wbuf.at[0], wbuf.at[4], f_l)
+    rest = pl.ds(n_pre, n_rest)
+    w_own_r = wcopy(1, wbuf.at[0, rest], wbuf.at[2, rest], f_r)
+    w_own_l = wcopy(2, wbuf.at[0, rest], wbuf.at[4, rest], f_l)
     w_2p = wcopy(3, wbuf.at[2], wbuf.at[3], f_p)
     w_4p = wcopy(4, wbuf.at[4], wbuf.at[5], f_p)
     w_2r = wcopy(5, wbuf.at[2, top], wbuf.at[6, top], f_r)
@@ -342,7 +453,7 @@
     w_own_r.start()
     w_own_l.start()
     w_own_p.start()
-    for c in ld_x:
+    for c in ld_x + ld_pre:
         c.wait()
 
     def block_of(k):
@@ -526,10 +637,10 @@
 MT = 512
 PART_SLOTS = 5
 LAND_SLOTS = 4
-GAP = 3
-
-
-def reduce_call(az, x, wo, wd):
+GAP = 1
+
+
+def reduce_call(az, pre, x, wo, wd):
     seq, kk = az.shape
     d = x.shape[1]
     cols = d // COL
@@ -541,7 +652,7 @@
     res = pl.pallas_call(
         reduce_kernel,
         out_shape=pltpu.VMEM((COL, seq, cols), bf),
-        in_specs=[vm, hbm, hbm, hbm],
+        in_specs=[vm, hbm, hbm, hbm, hbm],
         out_specs=vm,
         scratch_shapes=[
             pltpu.VMEM((COL, kk, cols), bf),
@@ -555,12 +666,12 @@
             pltpu.SemaphoreType.DMA((COL, 2, 2, 8)),
             pltpu.SemaphoreType.DMA((8,)),
             pltpu.SemaphoreType.DMA((8,)),
-            pltpu.SemaphoreType.DMA((4,)),
+            pltpu.SemaphoreType.DMA((6,)),
         ],
         compiler_params=pltpu.CompilerParams(collective_id=1, has_side_effects=True, vmem_limit_bytes=40 * 1024 * 1024),
         cost_estimate=pl.CostEstimate(flops=2 * seq * kk * d, bytes_accessed=4 * seq * d, transcendentals=0),
         name="down_reduce",
-    )(az, x, wo, wd)
+    )(az, pre, x, wo, wd)
     return write_out(res)[None]
 
 
@@ -590,8 +701,8 @@
     row_spec = P(("dp", "fsdp"), None, None)
 
     def local_layer(hidden, positions, norm_gain, w_query, w_key, w_value, w_gate, w_up, w_out, w_down):
-        az = project_call(hidden[0], positions, norm_gain, w_query, w_key, w_value, w_gate, w_up)
-        return reduce_call(az, hidden[0], w_out, w_down)
+        az, pre = project_call(hidden[0], positions, norm_gain, w_query, w_key, w_value, w_gate, w_up, w_out, w_down)
+        return reduce_call(az, pre, hidden[0], w_out, w_down)
 
     in_specs = (row_spec, P(None), P("fsdp"), P("fsdp", "tp"), P("fsdp", None), P("fsdp", None), P("fsdp", "tp"), P("fsdp", "tp"), P("tp", "fsdp"), P("tp", "fsdp"))
     return jax.shard_map(local_layer, mesh=mesh, in_specs=in_specs, out_specs=row_spec, check_vma=False)

time: 316 us -> 311 us (0.984)
  Pallas kernels: 315 us -> 311 us
    pallas_call x1, Pallas kernels: 195 us -> 187 us  [reduce_call(): pl.pallas_call(reduce_kernel, out_shape=pltpu.VMEM((COL, seq, cols), bf),...]
where the time goes in v4:
time: 311 us
  Pallas kernels  311 us (100%)
    pallas_call x1, Pallas kernels, reduce_call(): pl.pallas_call(reduce_kernel, out_shape=pltpu.VMEM((COL, seq, cols), bf),...  187 us
    pallas_call x1, Pallas kernels, project_call(): pl.pallas_call(project_kernel, out_shape=(jax.ShapeDtypeStruct((seq, hd +...  117 us

profile of v4, /device:TPU:0, one launch (start us, length us, event | category | flops | bytes accessed | tf_op | source)
XLA Modules:
  0.0 310.6 jit_solution(16428067949540204854)
XLA Ops:
  0.0 117.3 %gather_project.1 = (bf16[2048,1280]{1,0:T(8,128)(2,1)}, bf16[2,768,512]{2,1,0:T(8,128)(2,1)}) custom-call(bf16[2048,4096]{1,0:T(8,128)(2,1)} %bitcast.9, s32[16,128]{1,0:T(8,128)} %bitcast.16, f32[1,128]{1,0:T(1,128)} %constant.4.inv_freq, f32[1,512]{1,0:T(1,128)} %bitcast.17, bf16[4,4,32,256]{3,2,1,0:T(8,128)(2,1)} %bitcast.13, ...), custom_call_target="tpu_custom_call" | custom-call | flops 49392123904 | bytes 16777216 | tf_op jit(solution)/shard_map/gather_project/pallas_call | solution.py:360
  117.3 187.4 %down_reduce.1.src = bf16[8,2048,512]{2,1,0:T(8,128)(2,1)S(1)} custom-call(bf16[2048,1280]{1,0:T(8,128)(2,1)} %get-tuple-element.7.az, bf16[2,768,512]{2,1,0:T(8,128)(2,1)} %get-tuple-element.8.pre, bf16[2048,4096]{1,0:T(8,128)(2,1)} %bitcast.10, bf16[256,512]{1,0:T(8,128)(2,1)} %wo.3, bf16[1024,512]{1,0:T(8,128)(2,1)} %wd.3), custom_call_target="tpu_custom_call" | custom-call | flops 21474836480 | bytes 33554432 | tf_op jit(solution)/shard_map/down_reduce/pallas_call | solution.py:652
  304.7 5.9 %write_out.1 = bf16[2048,4096]{1,0:T(8,128)(2,1)} custom-call(bf16[8,2048,512]{2,1,0:T(8,128)(2,1)S(1)} %down_reduce.1.src), custom_call_target="tpu_custom_call" | custom-call | tf_op jit(solution)/shard_map/write_out/pallas_call | solution.py:689

commit v5 on v4

--- a/solution.py
+++ b/solution.py
@@ -33,10 +33,11 @@
 LN_SUB = 64
 GU = 128
 M1 = 1024
-PRE_DOWN = 512
-
-
-def project_kernel(x_hbm, pos, inv_freq, gain, wq, wk, wv, wg, wu, wo, wd, az, pre, wbuf, h, q, k, v, cos_t, sin_t, gbuf, xb, scores, acc,
+M2 = 512
+PRE_DOWN = 256
+
+
+def project_kernel(x_hbm, pos, inv_freq, gain, wq, wk, wv, wg, wu, wo, wd, az, pre, wbuf, h, q, kv, cos_t, sin_t, gbuf, xb, scores,
                    ssem, rsem, gss, grs, lsem, gsem, xsem, kss, krs, pss, prs):
     f = lax.axis_index("fsdp")
     nf = lax.axis_size("fsdp")
@@ -106,23 +107,34 @@
 
     kv_rings = ((ring_y, ring_z), (ring_z, ring_y))
 
-    def kv_unit(i, dev, lo, n):
-        z, y = (z_id, dev) if i == 0 else (dev, y_id)
-        return wbuf.at[1 + i, pl.ds(lo, n), z, y]
-
-    def kv_line(i, dev, lo, n):
+    def ids_of(i, dev):
+        return (z_id, dev) if i == 0 else (dev, y_id)
+
+    def w_view(i, line, dev, part):
+        lo, n = ((0, nf), (0, nf // 2), (nf // 2, nf // 2))[part]
+        if not line:
+            z, y = ids_of(i, dev)
+            return wbuf.at[1 + i, pl.ds(lo, n), z, y]
         return wbuf.at[1 + i, pl.ds(lo, n), dev] if i == 0 else wbuf.at[1 + i, pl.ds(lo, n), :, dev]
+
+    def o_view(i, line, dev, part):
+        size = TPA if line else kv.shape[3]
+        lo, n = ((0, size), (0, size // 2), (size // 2, size // 2))[part]
+        if not line:
+            z, y = ids_of(i, dev)
+            return kv.at[i, z, y, pl.ds(lo, n)]
+        return kv.at[i, dev, pl.ds(lo, n)] if i == 0 else kv.at[i, pl.ds(lo, n), dev]
 
     def kv_copies(step):
         res = []
+        view = w_view if step < 4 else o_view
         for i in range(2):
-            ids = kv_rings[i][step // 2]
-            me, r, l = ids
-            view = kv_line if step >= 2 else kv_unit
+            me, r, l = kv_rings[i][step // 2 % 2]
+            line = step // 2 % 2 == 1
             if step % 2 == 0:
-                src = (view(i, me, 0, nf), view(i, me, 0, nf))
+                src = (view(i, line, me, 0), view(i, line, me, 0))
             else:
-                src = (view(i, (me + TPA - 1) % TPA, 0, nf // 2), view(i, (me + 1) % TPA, nf // 2, nf // 2))
+                src = (view(i, line, (me + TPA - 1) % TPA, 1), view(i, line, (me + 1) % TPA, 2))
             for d_, (part, dev) in enumerate(zip(src, (r, l))):
                 res.append(pltpu.make_async_remote_copy(src_ref=part, dst_ref=part, send_sem=kss.at[nf + step, 2 * i + d_], recv_sem=krs.at[nf + step, 2 * i + d_],
                                                         device_id={"tp": dev}, device_id_type=MESH))
@@ -240,54 +252,58 @@
                 out = centered * lax.rsqrt(var + NORM_EPS) * gbuf[...]
                 h[pl.ds(pl.multiple_of(blk * LN_ROWS + r * LN_SUB, LN_SUB), LN_SUB), :] = out.astype(jnp.bfloat16)
 
-    norm_blocks(0, n_blk // 2)
-    net_a(0)
+    norm_blocks(0, n_blk // 4)
     kv_finish(0)
     kv_start(1)
-    norm_blocks(n_blk // 2, n_blk)
+    norm_blocks(n_blk // 4, n_blk // 2)
+    net_a(0)
     kv_finish(1)
     kv_start(2)
-
-    def rope(rows):
-        y = acc[...].astype(jnp.bfloat16).astype(jnp.float32)
-        a, b = y[:, :hd // 2], y[:, hd // 2:]
+    norm_blocks(n_blk // 2, n_blk)
+
+    def product(i, rows):
+        return jnp.dot(h[rows, :], wbuf[i].reshape(d, hd), preferred_element_type=jnp.float32)
+
+    def rope(y, rows):
+        a, b = y[:, :hd // 2].astype(jnp.bfloat16).astype(jnp.float32), y[:, hd // 2:].astype(jnp.bfloat16).astype(jnp.float32)
         c, s = cos_t[rows, :], sin_t[rows, :]
         return jnp.concatenate([a * c - b * s, b * c + a * s], axis=1).astype(jnp.bfloat16)
 
+    def keys_values():
+        n = kv.shape[3]
+        rows = pl.ds(pl.multiple_of(t * n, n), n)
+        kv[0, z_id, y_id] = rope(product(1, rows), rows)
+        kv[1, z_id, y_id] = product(2, rows).astype(jnp.bfloat16)
+
     def compute(i):
-        @pl.loop(0, seq // M1)
-        def _(m):
-            rows = pl.ds(pl.multiple_of(m * M1, M1), M1)
-            acc[...] = jnp.dot(h[rows, :], wbuf[i].reshape(d, hd), preferred_element_type=jnp.float32)
-
-            @pl.when(i == 0)
-            def _():
-                q[rows, :] = rope(rows)
-
-            @pl.when(i == 1)
-            def _():
-                k[rows, :] = rope(rows)
-
-            @pl.when(i == 2)
-            def _():
-                v[rows, :] = acc[...].astype(jnp.bfloat16)
-
-            @pl.when(i >= 3)
-            def _():
-                g = acc[:, :GU].astype(jnp.bfloat16).astype(jnp.float32)
-                u = acc[:, GU:].astype(jnp.bfloat16).astype(jnp.float32)
+        @pl.when(i == 0)
+        def _():
+            @pl.loop(0, seq // M1)
+            def _(m):
+                rows = pl.ds(pl.multiple_of(m * M1, M1), M1)
+                q[rows, :] = rope(product(i, rows), rows)
+
+        @pl.when(i >= 3)
+        def _():
+            for m in range(seq // M2):
+                rows = pl.ds(m * M2, M2)
+                y = product(i, rows)
+                g = y[:, :GU].astype(jnp.bfloat16).astype(jnp.float32)
+                u = y[:, GU:].astype(jnp.bfloat16).astype(jnp.float32)
                 z = (g * (1.0 / (1.0 + jnp.exp(-g)))) * u
                 az[rows, pl.ds(pl.multiple_of(hd + (i - 3) * GU, GU), GU)] = z.astype(jnp.bfloat16)
 
     scale = hd ** -0.5
     n_q = seq // QB
+
+    keys, values = (kv.at[i].reshape(seq, hd) for i in range(2))
 
     def attend(b):
         rows = pl.ds(b * QB, QB)
         qb = q[rows, :]
         peak = None
         for t in range(b + 1):
-            s = lax.dot_general(qb, k[pl.ds(t * QB, QB), :], (((1,), (1,)), ((), ())), preferred_element_type=jnp.float32) * scale
+            s = lax.dot_general(qb, keys[pl.ds(t * QB, QB), :], (((1,), (1,)), ((), ())), preferred_element_type=jnp.float32) * scale
             if t == b:
                 keep = lax.broadcasted_iota(jnp.int32, (QB, QB), 1) <= lax.broadcasted_iota(jnp.int32, (QB, QB), 0)
                 s = jnp.where(keep, s, -1e30)
@@ -303,45 +319,46 @@
             total = e if total is None else total + e
         inv = 1.0 / jnp.sum(total, axis=-1, keepdims=True)
         p = (scores[:, :(b + 1) * QB] * inv).astype(jnp.bfloat16)
-        out = jnp.dot(p, v[pl.ds(0, (b + 1) * QB), :], preferred_element_type=jnp.float32)
+        out = jnp.dot(p, values[pl.ds(0, (b + 1) * QB), :], preferred_element_type=jnp.float32)
         az[rows, 0:hd] = out.astype(jnp.bfloat16)
 
-    n_first = 3
-
-    @pl.loop(0, n_chunk)
+    @pl.loop(0, n_x)
     def _(j):
-        on_k, on_v = j == n_first + 1, j == n_first + 3
-        xi = j - (j + n_chunk - n_first - 1) // n_chunk - (j + n_chunk - n_first - 3) // n_chunk
-        on_x = jnp.logical_not(jnp.logical_or(on_k, on_v))
-
-        @pl.when(on_x)
-        def _():
-            @pl.when(xi + 1 < n_x)
-            def _():
-                net_a(xi + 1)
-
-            net_b(xi)
-
-        @pl.when(j == 2)
+        @pl.when(j + 1 < n_x)
+        def _():
+            net_a(j + 1)
+
+        net_b(j)
+
+        @pl.when(j == 1)
         def _():
             kv_finish(2)
             kv_start(3)
 
-        @pl.when(on_k)
+        @pl.when(j == 2)
         def _():
             kv_finish(3)
-
-        for lo, hi, step in ((0, 4, n_first + 4), (4, 6, n_first + 5), (6, 8, n_first + 6)):
+            keys_values()
+            kv_start(4)
+
+        for step in range(4, 7):
+            @pl.when(j == step - 1)
+            def _(step=step):
+                kv_finish(step)
+                kv_start(step + 1)
+
+        @pl.when(j == n_x - 3)
+        def _():
+            kv_finish(7)
+
+        for lo, hi, step in ((0, 5, n_x - 3), (5, 8, n_x - 2)):
             @pl.when(j == step)
             def _(lo=lo, hi=hi):
                 for b in range(lo, hi):
                     attend(b)
 
-        @pl.when(on_x)
-        def _():
-            ready(chunk_of(xi))
-
-        compute(jnp.where(on_k, 1, jnp.where(on_v, 2, chunk_of(xi))))
+        ready(chunk_of(j))
+        compute(chunk_of(j))
 
     for c in pre_copies():
         c.wait()
@@ -366,14 +383,12 @@
             pltpu.VMEM((n_chunk, d // depth, TPA, TPA, depth // TPA // TPA, hd), bf),
             pltpu.VMEM((seq, d), bf),
             pltpu.VMEM((seq, hd), bf),
-            pltpu.VMEM((seq, hd), bf),
-            pltpu.VMEM((seq, hd), bf),
+            pltpu.VMEM((2, TPA, TPA, seq // TPA // TPA, hd), bf),
             pltpu.VMEM((seq, hd // 2), f32),
             pltpu.VMEM((seq, hd // 2), f32),
             pltpu.VMEM((1, d), f32),
             pltpu.VMEM((X_SLOTS, LN_ROWS, d), bf),
             pltpu.VMEM((QB, seq), f32),
-            pltpu.VMEM((M1, hd), f32),
             pltpu.SemaphoreType.DMA((n_chunk, 8)),
             pltpu.SemaphoreType.DMA((n_chunk, 8)),
             pltpu.SemaphoreType.DMA((8,)),
@@ -381,8 +396,8 @@
             pltpu.SemaphoreType.DMA((n_chunk, 2)),
             pltpu.SemaphoreType.DMA,
             pltpu.SemaphoreType.DMA((X_SLOTS,)),
-            pltpu.SemaphoreType.DMA((12, 4)),
-            pltpu.SemaphoreType.DMA((12, 4)),
+            pltpu.SemaphoreType.DMA((16, 4)),
+            pltpu.SemaphoreType.DMA((16, 4)),
             pltpu.SemaphoreType.DMA((2, 2)),
             pltpu.SemaphoreType.DMA((2, 2)),
         ],

time: 311 us -> 299 us (0.961)
  Pallas kernels: 311 us -> 298 us
    pallas_call x1, Pallas kernels: 117 us -> 107 us  [project_call(): pl.pallas_call(project_kernel, out_shape=(jax.ShapeDtypeStruct((seq, hd +...]
where the time goes in v5:
time: 299 us; the launch traced here: 298 us
  Pallas kernels  298 us (100%)
    pallas_call x1, Pallas kernels, reduce_call(): pl.pallas_call(reduce_kernel, out_shape=pltpu.VMEM((COL, seq, cols), bf),...  185 us
    pallas_call x1, Pallas kernels, project_call(): pl.pallas_call(project_kernel, out_shape=(jax.ShapeDtypeStruct((seq, hd +...  107 us

profile of v5, /device:TPU:0, one launch (start us, length us, event | category | flops | bytes accessed | tf_op | source)
XLA Modules:
  0.0 298.4 jit_solution(8329738773020883426)
XLA Ops:
  0.0 107.1 %gather_project.1 = (bf16[2048,1280]{1,0:T(8,128)(2,1)}, bf16[2,512,512]{2,1,0:T(8,128)(2,1)}) custom-call(bf16[2048,4096]{1,0:T(8,128)(2,1)} %bitcast.9, s32[16,128]{1,0:T(8,128)} %bitcast.16, f32[1,128]{1,0:T(1,128)} %constant.4.inv_freq, f32[1,512]{1,0:T(1,128)} %bitcast.17, bf16[4,4,32,256]{3,2,1,0:T(8,128)(2,1)} %bitcast.13, ...), custom_call_target="tpu_custom_call" | custom-call | flops 49392123904 | bytes 16777216 | tf_op jit(solution)/shard_map/gather_project/pallas_call | solution.py:377
  107.1 185.2 %down_reduce.1.src = bf16[8,2048,512]{2,1,0:T(8,128)(2,1)S(1)} custom-call(bf16[2048,1280]{1,0:T(8,128)(2,1)} %get-tuple-element.7.az, bf16[2,512,512]{2,1,0:T(8,128)(2,1)} %get-tuple-element.8.pre, bf16[2048,4096]{1,0:T(8,128)(2,1)} %bitcast.10, bf16[256,512]{1,0:T(8,128)(2,1)} %wo.3, bf16[1024,512]{1,0:T(8,128)(2,1)} %wd.3), custom_call_target="tpu_custom_call" | custom-call | flops 21474836480 | bytes 33554432 | tf_op jit(solution)/shard_map/down_reduce/pallas_call | solution.py:667
  292.3 5.9 %write_out.1 = bf16[2048,4096]{1,0:T(8,128)(2,1)} custom-call(bf16[8,2048,512]{2,1,0:T(8,128)(2,1)S(1)} %down_reduce.1.src), custom_call_target="tpu_custom_call" | custom-call | tf_op jit(solution)/shard_map/write_out/pallas_call | solution.py:704

commit v6 on v5

--- a/solution.py
+++ b/solution.py
@@ -29,16 +29,16 @@
 
 QB = 256
 LN_ROWS = 128
-X_SLOTS = 4
+X_SLOTS = 3
 LN_SUB = 64
 GU = 128
 M1 = 1024
 M2 = 512
-PRE_DOWN = 256
-
-
-def project_kernel(x_hbm, pos, inv_freq, gain, wq, wk, wv, wg, wu, wo, wd, az, pre, wbuf, h, q, kv, cos_t, sin_t, gbuf, xb, scores,
-                   ssem, rsem, gss, grs, lsem, gsem, xsem, kss, krs, pss, prs):
+VMEM_LIMIT = 95 * 512 * 1024
+
+
+def project_part(x_hbm, pos, inv_freq, gain, wq, wk, wv, wg, wu, az, wbuf, h, q, kv, cos_t, sin_t, gbuf, xb, scores,
+                 ssem, rsem, gss, grs, lsem, gsem, xsem, kss, krs, send_late):
     f = lax.axis_index("fsdp")
     nf = lax.axis_size("fsdp")
     t = lax.axis_index("tp")
@@ -149,17 +149,6 @@
             c.wait_recv()
             c.wait_send()
 
-    n_o = wo.shape[0]
-    n_d = pre.shape[1] - n_o
-
-    def pre_copies():
-        res = []
-        for d_, dev in ((0, f_r), (1, f_l)):
-            for e, (src, lo, n) in enumerate(((wo, 0, n_o), (wd, n_o, n_d))):
-                res.append(pltpu.make_async_remote_copy(src_ref=src.at[pl.ds(0, n)], dst_ref=pre.at[d_, pl.ds(lo, n)], send_sem=pss.at[d_, e], recv_sem=prs.at[d_, e],
-                                                        device_id={"fsdp": dev}, device_id_type=MESH))
-        return res
-
     def send_own(i):
         for part in range(2):
             load(i, part, wq, part * GU).wait()
@@ -179,8 +168,7 @@
 
         @pl.when(xi + 1 == n_x)
         def _():
-            for c in pre_copies():
-                c.start()
+            send_late()
 
         transfer(i, 5).start()
         transfer(i, 6).start()
@@ -360,121 +348,105 @@
         ready(chunk_of(j))
         compute(chunk_of(j))
 
-    for c in pre_copies():
-        c.wait()
-
-
-def project_call(x, positions, norm_gain, w_query, w_key, w_value, w_gate, w_up, w_out, w_down):
-    seq, d = x.shape
-    depth, hd = w_query.shape
-    ff = w_gate.shape[1]
-    n_chunk = 3 + ff // GU
-    inv_freq = jnp.asarray((10000.0 ** (-np.arange(0, hd, 2) / hd)).astype(np.float32))
-    bf, f32 = jnp.bfloat16, jnp.float32
-    hbm = pl.BlockSpec(memory_space=pl.ANY)
-    vm = pl.BlockSpec(memory_space=pltpu.VMEM)
-    flops = 2 * seq * d * (3 * hd + 2 * ff) + 2 * seq * seq * hd
-    return pl.pallas_call(
-        project_kernel,
-        out_shape=(jax.ShapeDtypeStruct((seq, hd + ff), bf), jax.ShapeDtypeStruct((2, hd + PRE_DOWN, w_out.shape[1]), bf)),
-        in_specs=[hbm, vm, vm] + [hbm] * 8,
-        out_specs=(vm, hbm),
-        scratch_shapes=[
-            pltpu.VMEM((n_chunk, d // depth, TPA, TPA, depth // TPA // TPA, hd), bf),
-            pltpu.VMEM((seq, d), bf),
-            pltpu.VMEM((seq, hd), bf),
-            pltpu.VMEM((2, TPA, TPA, seq // TPA // TPA, hd), bf),
-            pltpu.VMEM((seq, hd // 2), f32),
-            pltpu.VMEM((seq, hd // 2), f32),
-            pltpu.VMEM((1, d), f32),
-            pltpu.VMEM((X_SLOTS, LN_ROWS, d), bf),
-            pltpu.VMEM((QB, seq), f32),
-            pltpu.SemaphoreType.DMA((n_chunk, 8)),
-            pltpu.SemaphoreType.DMA((n_chunk, 8)),
-            pltpu.SemaphoreType.DMA((8,)),
-            pltpu.SemaphoreType.DMA((8,)),
-            pltpu.SemaphoreType.DMA((n_chunk, 2)),
-            pltpu.SemaphoreType.DMA,
-            pltpu.SemaphoreType.DMA((X_SLOTS,)),
-            pltpu.SemaphoreType.DMA((16, 4)),
-            pltpu.SemaphoreType.DMA((16, 4)),
-            pltpu.SemaphoreType.DMA((2, 2)),
-            pltpu.SemaphoreType.DMA((2, 2)),
-        ],
-        compiler_params=pltpu.CompilerParams(collective_id=0, has_side_effects=True, vmem_limit_bytes=63 * 1024 * 1024),
-        cost_estimate=pl.CostEstimate(flops=flops, bytes_accessed=2 * seq * d, transcendentals=0),
-        name="gather_project",
-    )(x, positions.reshape(seq // 128, 128), inv_freq.reshape(1, hd // 2), norm_gain.reshape(1, depth),
-      *(w.reshape(TPA, TPA, depth // TPA // TPA, w.shape[1]) for w in (w_query, w_key, w_value, w_gate, w_up)), w_out, w_down)
-
-
-def reduce_kernel(az, pre, x_hbm, wo, wd, out, wbuf, part, r1, r2, r3, r4, xbuf,
-                  ssem, rsem, wss, wrs, lsem):
+
+def reduce_part(az, x_hbm, wo, wd, out, w2, wbuf, wvm, xb, ssem, rsem, wss, wrs, lsem, xsem, phase):
     t = lax.axis_index("tp")
     f = lax.axis_index("fsdp")
     ring_y, ring_z = _ring_ids(t)
     xc, core, f_p, f_r, f_l = _fsdp_ids(f)
     seq = az.shape[0]
-    cols = wbuf.shape[2]
+    cols = wvm.shape[2]
+    part = wbuf.at[pl.ds(0, 5)].reshape(5, 2, seq, cols // 2)
     half = seq // 2
     big = half // TPA
     small = big // TPA
+    r2 = wbuf.at[pl.ds(5, 2)].reshape(LAND_SLOTS, 2, 2, 2, big, cols // 2)
+    r1 = wbuf.at[pl.ds(7, 2)].reshape(COL, 2, 2, 2, big // 2, cols // 2)
+    r4 = wbuf.at[9].reshape(COL, 2, 2, 2, small, cols // 2)
+    r3 = wbuf.at[10, pl.ds(0, 4)].reshape(COL, 2, 2, 2, small // 2, cols // 2)
     hd = wo.shape[0]
 
-    ld_o = pltpu.make_async_copy(wo, wbuf.at[0, pl.ds(0, hd)], lsem.at[0])
-    ld_d = pltpu.make_async_copy(wd, wbuf.at[0, pl.ds(hd, wd.shape[0])], lsem.at[1])
-    n_pre = pre.shape[1]
-    n_rest = wbuf.shape[1] - n_pre
-    ld_pre = [pltpu.make_async_copy(pre.at[e], wbuf.at[2 + 2 * e, pl.ds(0, n_pre)], lsem.at[4 + e]) for e in range(2)]
-    ld_o.start()
-    ld_d.start()
-    for c in ld_pre:
-        c.start()
     axes = ((ring_y, ring_z), (ring_z, ring_y))
 
     def own_rows(h):
         (i1, _, _), (i2, _, _) = axes[h]
         return pl.multiple_of(h * half + i1 * big + i2 * small, small)
 
-    ld_x = [pltpu.make_async_copy(x_hbm.at[pl.ds(own_rows(h), small), :], xbuf.at[h], lsem.at[2 + h]) for h in range(2)]
-    for c in ld_x:
-        c.start()
-
-    barrier = pltpu.get_barrier_semaphore()
-    for other in (ring_y[1], ring_y[2], ring_z[1], ring_z[2]):
-        pl.semaphore_signal(barrier, inc=1, device_id={"tp": other}, device_id_type=MESH)
-    for other in (f_p, f_r, f_l):
-        pl.semaphore_signal(barrier, inc=1, device_id={"fsdp": other}, device_id_type=MESH)
-    pl.semaphore_wait(barrier, 7)
-
-    def wcopy(k, src, dst, dev):
-        return pltpu.make_async_remote_copy(src_ref=src, dst_ref=dst, send_sem=wss.at[k], recv_sem=wrs.at[k],
+    xrow = [xb.at[0, pl.ds(hf * small, small)] for hf in range(2)]
+    ld_x = [pltpu.make_async_copy(x_hbm.at[pl.ds(own_rows(hf), small), :], xrow[hf], xsem.at[hf]) for hf in range(2)]
+
+    def wcopy(k, e, src, dst, dev):
+        return pltpu.make_async_remote_copy(src_ref=src, dst_ref=dst, send_sem=wss.at[k, e], recv_sem=wrs.at[k, e],
                                             device_id={"fsdp": dev}, device_id_type=MESH)
 
-    kk = wbuf.shape[1]
+    kk = wvm.shape[1]
     kh = kk // 2
-    top, bot = pl.ds(0, kh), pl.ds(kh, kh)
-    w_own_p = wcopy(0, wbuf.at[0], wbuf.at[1], f_p)
-    rest = pl.ds(n_pre, n_rest)
-    w_own_r = wcopy(1, wbuf.at[0, rest], wbuf.at[2, rest], f_r)
-    w_own_l = wcopy(2, wbuf.at[0, rest], wbuf.at[4, rest], f_l)
-    w_2p = wcopy(3, wbuf.at[2], wbuf.at[3], f_p)
-    w_4p = wcopy(4, wbuf.at[4], wbuf.at[5], f_p)
-    w_2r = wcopy(5, wbuf.at[2, top], wbuf.at[6, top], f_r)
-    w_4l = wcopy(6, wbuf.at[4, bot], wbuf.at[6, bot], f_l)
-    w_6p = wcopy(7, wbuf.at[6], wbuf.at[7], f_p)
-    ld_o.wait()
-    ld_d.wait()
-    w_own_r.start()
-    w_own_l.start()
-    w_own_p.start()
-    for c in ld_x + ld_pre:
-        c.wait()
+    rows_o, rows_d = pl.ds(0, hd), pl.ds(hd, kk - hd)
+
+    def w_own(k, slot, dev):
+        return wcopy(k, 0, wo, w2.at[slot, rows_o], dev), wcopy(k, 1, wd, w2.at[slot, rows_d], dev)
+
+    def w_whole(k, slot):
+        return wcopy(k, 0, w2.at[slot], w2.at[slot + 1], f_p)
+
+    def w_2r():
+        return wcopy(5, 0, w2.at[2, pl.ds(0, kh)], w2.at[6, pl.ds(0, kh)], f_r)
+
+    def w_4l():
+        return wcopy(6, 0, w2.at[4, pl.ds(kh, kh)], w2.at[6, pl.ds(kh, kh)], f_l)
+
+    def load_own():
+        return (pltpu.make_async_copy(wo, wvm.at[0, rows_o], lsem.at[2]), pltpu.make_async_copy(wd, wvm.at[0, rows_d], lsem.at[3]))
+
+    def load_w(cb):
+        return pltpu.make_async_copy(w2.at[cb], wvm.at[cb % 2], lsem.at[cb % 2])
+
+    def send_late():
+        for c in w_own(1, 2, f_r) + w_own(2, 4, f_l) + w_own(0, 1, f_p) + load_own():
+            c.start()
+
+    def fetch(cb):
+        @pl.when(cb == 1)
+        def _():
+            for c in w_own(0, 1, f_p):
+                c.wait()
+
+        @pl.when(cb == 2)
+        def _():
+            for c in w_own(1, 2, f_r) + w_own(2, 4, f_l):
+                c.wait()
+            w_2r().start()
+            w_4l().start()
+            w_whole(3, 2).start()
+            w_whole(4, 4).start()
+
+        @pl.when(cb == 3)
+        def _():
+            w_whole(3, 2).wait()
+
+        @pl.when(cb == 5)
+        def _():
+            w_whole(4, 4).wait()
+
+        @pl.when(cb == 6)
+        def _():
+            w_2r().wait()
+            w_4l().wait()
+            w_whole(7, 6).start()
+
+        @pl.when(cb == 7)
+        def _():
+            w_whole(7, 6).wait()
+
+        load_w(cb).start()
 
     def block_of(k):
         q = k // 2
         dx = 3 * q - 5 * (q // 2) - 2 * (q // 3)
         return ((xc + dx) % 4) * 2 + (core + k % 2) % 2
+
+    def block_cols(cb):
+        return pl.ds(pl.multiple_of(block_of(cb) * cols, cols), cols)
 
     def ring_copy(cb, h, d, step, src, dst, dev):
         return pltpu.make_async_remote_copy(src_ref=src, dst_ref=dst, send_sem=ssem.at[cb, h, d, step],
@@ -485,15 +457,15 @@
         o = (i + 2) % TPA
         m = n // 2
         s = pl.multiple_of(base + o * n, m)
-        return (ring_copy(cb, h, 0, step, part.at[cb % PART_SLOTS, pl.ds(s, m)], land.at[cb % land.shape[0], h, 0], r),
-                ring_copy(cb, h, 1, step, part.at[cb % PART_SLOTS, pl.ds(s + m, m)], land.at[cb % land.shape[0], h, 1], l))
+        return (ring_copy(cb, h, 0, step, part.at[cb % PART_SLOTS, :, pl.ds(s, m)], land.at[cb % land.shape[0], h, 0], r),
+                ring_copy(cb, h, 1, step, part.at[cb % PART_SLOTS, :, pl.ds(s + m, m)], land.at[cb % land.shape[0], h, 1], l))
 
     def rs_second(cb, h, step, ring, base, n, land):
         i, r, l = ring
         s_r = pl.multiple_of(base + ((i + 1) % TPA) * n, n)
         s_l = pl.multiple_of(base + ((i + 3) % TPA) * n, n)
-        return (ring_copy(cb, h, 0, step, part.at[cb % PART_SLOTS, pl.ds(s_r, n)], land.at[cb % land.shape[0], h, 0], r),
-                ring_copy(cb, h, 1, step, part.at[cb % PART_SLOTS, pl.ds(s_l, n)], land.at[cb % land.shape[0], h, 1], l))
+        return (ring_copy(cb, h, 0, step, part.at[cb % PART_SLOTS, :, pl.ds(s_r, n)], land.at[cb % land.shape[0], h, 0], r),
+                ring_copy(cb, h, 1, step, part.at[cb % PART_SLOTS, :, pl.ds(s_l, n)], land.at[cb % land.shape[0], h, 1], l))
 
     def rs_update(cb, h, ring, base, n, land):
         i, _, _ = ring
@@ -502,22 +474,20 @@
         s_l = pl.multiple_of(base + ((i + 3) % TPA) * n + m, m)
         for s, d in ((s_r, 0), (s_l, 1)):
             rows = pl.ds(s, m)
-            part[cb % PART_SLOTS, rows] = (part[cb % PART_SLOTS, rows].astype(jnp.float32) + land[cb % land.shape[0], h, d].astype(jnp.float32)).astype(jnp.bfloat16)
+            part[cb % PART_SLOTS, :, rows] = (part[cb % PART_SLOTS, :, rows].astype(jnp.float32) + land[cb % land.shape[0], h, d].astype(jnp.float32)).astype(jnp.bfloat16)
 
     def ag_first(cb, h, step, ring, src, base, n):
         i, r, l = ring
-        g = block_of(cb)
-        dst = out.at[g, pl.ds(pl.multiple_of(base + i * n, n), n)]
+        dst = out.at[pl.ds(pl.multiple_of(base + i * n, n), n), block_cols(cb)]
         if src is None:
             src = dst
         return (ring_copy(cb, h, 0, step, src, dst, r), ring_copy(cb, h, 1, step, src, dst, l))
 
     def ag_second(cb, h, step, ring, base, n):
         i, r, l = ring
-        g = block_of(cb)
         m = n // 2
-        from_l = out.at[g, pl.ds(pl.multiple_of(base + ((i + 3) % TPA) * n, m), m)]
-        from_r = out.at[g, pl.ds(pl.multiple_of(base + ((i + 1) % TPA) * n + m, m), m)]
+        from_l = out.at[pl.ds(pl.multiple_of(base + ((i + 3) % TPA) * n, m), m), block_cols(cb)]
+        from_r = out.at[pl.ds(pl.multiple_of(base + ((i + 1) % TPA) * n + m, m), m), block_cols(cb)]
         return (ring_copy(cb, h, 0, step, from_l, from_l, r), ring_copy(cb, h, 1, step, from_r, from_r, l))
 
     def copies(cb, step):
@@ -554,41 +524,25 @@
             c.wait_send()
 
     def stage0(cb):
-        @pl.when(cb == 1)
-        def _():
-            w_own_p.wait()
-
-        @pl.when(cb == 2)
-        def _():
-            w_own_r.wait()
-            w_own_l.wait()
-            w_2r.start()
-            w_4l.start()
-            w_2p.start()
-            w_4p.start()
-
-        @pl.when(cb == 3)
-        def _():
-            w_2p.wait()
-
-        @pl.when(cb == 5)
-        def _():
-            w_4p.wait()
-
-        @pl.when(cb == 6)
-        def _():
-            w_2r.wait()
-            w_4l.wait()
-            w_6p.start()
-
-        @pl.when(cb == 7)
-        def _():
-            w_6p.wait()
+        @pl.when(cb == 0)
+        def _():
+            for c in load_own():
+                c.wait()
+
+        @pl.when(cb > 0)
+        def _():
+            load_w(cb).wait()
 
         @pl.loop(0, seq // MT)
         def _(i):
             rows = pl.ds(pl.multiple_of(i * MT, MT), MT)
-            part[cb % PART_SLOTS, rows] = jnp.dot(az[rows, :], wbuf[cb], preferred_element_type=jnp.float32).astype(jnp.bfloat16)
+            y = jnp.dot(az[rows, :], wvm[cb % 2], preferred_element_type=jnp.float32).astype(jnp.bfloat16)
+            for hf in range(2):
+                part[cb % PART_SLOTS, hf, rows] = y[:, hf * (cols // 2):(hf + 1) * (cols // 2)]
+
+        @pl.when(cb == 0)
+        def _():
+            pl.semaphore_wait(phase, 4)
 
         start(cb, 0)
 
@@ -602,7 +556,7 @@
         finish(cb, 1)
         for h in range(2):
             rows = pl.ds(pl.multiple_of(h * half + axes[h][0][0] * big, big), big)
-            part[cb % PART_SLOTS, rows] = (part[cb % PART_SLOTS, rows].astype(jnp.float32) + r2[cb % r2.shape[0], h, 0].astype(jnp.float32)
+            part[cb % PART_SLOTS, :, rows] = (part[cb % PART_SLOTS, :, rows].astype(jnp.float32) + r2[cb % r2.shape[0], h, 0].astype(jnp.float32)
                               + r2[cb % r2.shape[0], h, 1].astype(jnp.float32)).astype(jnp.bfloat16)
         start(cb, 2)
 
@@ -616,10 +570,12 @@
         finish(cb, 3)
         g = block_of(cb)
         for h in range(2):
-            branch = (part[cb % PART_SLOTS, pl.ds(own_rows(h), small)].astype(jnp.float32) + r4[cb % r4.shape[0], h, 0].astype(jnp.float32)
+            branch = (part[cb % PART_SLOTS, :, pl.ds(own_rows(h), small)].astype(jnp.float32) + r4[cb % r4.shape[0], h, 0].astype(jnp.float32)
                       + r4[cb % r4.shape[0], h, 1].astype(jnp.float32))
-            xs = xbuf[h, :, pl.ds(pl.multiple_of(g * cols, cols), cols)].astype(jnp.float32)
-            out[g, pl.ds(own_rows(h), small), :] = (xs + branch).astype(jnp.bfloat16)
+            for hf in range(2):
+                lanes = pl.ds(pl.multiple_of(g * cols + hf * (cols // 2), cols // 2), cols // 2)
+                xs = xb[0, pl.ds(h * small, small), lanes].astype(jnp.float32)
+                out[pl.ds(own_rows(h), small), lanes] = (xs + branch[hf]).astype(jnp.bfloat16)
         start(cb, 4)
 
     def stage5(cb):
@@ -639,85 +595,122 @@
 
     stages = (stage0, stage1, stage2, stage3, stage4, stage5, stage6, stage7, stage8)
 
-    @pl.loop(0, COL + GAP + len(stages) - 1)
-    def _(n):
-        for s, fn in enumerate(stages):
-            turn = n - s
-
-            @pl.when(jnp.logical_or(jnp.logical_and(turn >= 0, turn < 2), jnp.logical_and(turn >= 2 + GAP, turn < COL + GAP)))
-            def _(fn=fn, turn=turn):
-                fn(jnp.where(turn >= 2, turn - GAP, turn))
+    def reduce_all():
+        for c in ld_x:
+            c.start()
+        for other in (ring_y[1], ring_y[2], ring_z[1], ring_z[2]):
+            pl.semaphore_signal(phase, inc=1, device_id={"tp": other}, device_id_type=MESH)
+        for c in ld_x:
+            c.wait()
+
+        @pl.loop(0, COL + len(stages) - 1)
+        def _(n):
+            for s, fn in enumerate(stages):
+                cb = n - s
+
+                @pl.when(jnp.logical_and(cb >= 0, cb < COL))
+                def _(fn=fn, cb=cb):
+                    fn(cb)
+
+            @pl.when(n + 1 < COL)
+            def _():
+                fetch(n + 1)
+
+    return send_late, reduce_all
 
 
 MT = 512
 PART_SLOTS = 5
 LAND_SLOTS = 4
-GAP = 1
-
-
-def reduce_call(az, pre, x, wo, wd):
-    seq, kk = az.shape
-    d = x.shape[1]
+
+
+def layer_kernel(x_hbm, pos, inv_freq, gain, wq, wk, wv, wg, wu, wo, wd, out, w2, wbuf, q, kv, cos_t, sin_t, gbuf, xb, scores, az, wvm,
+                 ssem, rsem, gss, grs, lsem, gsem, xsem, kss, krs, rss, rrs, wss, wrs, wlsem, phase):
+    send_late, reduce_all = reduce_part(az, x_hbm, wo, wd, out, w2, wbuf, wvm, xb, rss, rrs, wss, wrs, wlsem, xsem, phase)
+    project_part(x_hbm, pos, inv_freq, gain, wq, wk, wv, wg, wu, az, wbuf, out, q, kv, cos_t, sin_t, gbuf, xb, scores,
+                 ssem, rsem, gss, grs, lsem, gsem, xsem, kss, krs, send_late)
+    reduce_all()
+
+
+def layer_call(x, positions, norm_gain, w_query, w_key, w_value, w_gate, w_up, w_out, w_down):
+    seq, d = x.shape
+    depth, hd = w_query.shape
+    ff = w_gate.shape[1]
+    n_chunk = 3 + ff // GU
     cols = d // COL
-    half = seq // 2
-    big, small = half // TPA, half // TPA // TPA
-    bf = jnp.bfloat16
+    inv_freq = jnp.asarray((10000.0 ** (-np.arange(0, hd, 2) / hd)).astype(np.float32))
+    bf, f32 = jnp.bfloat16, jnp.float32
     hbm = pl.BlockSpec(memory_space=pl.ANY)
     vm = pl.BlockSpec(memory_space=pltpu.VMEM)
-    res = pl.pallas_call(
-        reduce_kernel,
-        out_shape=pltpu.VMEM((COL, seq, cols), bf),
-        in_specs=[vm, hbm, hbm, hbm, hbm],
-        out_specs=vm,
+    dma = pltpu.SemaphoreType.DMA
+    flops = 2 * seq * d * (3 * hd + 2 * ff) + 2 * seq * seq * hd + 2 * seq * d * (hd + ff)
+    return pl.pallas_call(
+        layer_kernel,
+        out_shape=(pltpu.VMEM((seq, d), bf), jax.ShapeDtypeStruct((COL, hd + ff, cols), bf)),
+        in_specs=[hbm, vm, vm] + [hbm] * 8,
+        out_specs=(vm, hbm),
         scratch_shapes=[
-            pltpu.VMEM((COL, kk, cols), bf),
-            pltpu.VMEM((PART_SLOTS, seq, cols), bf),
-            pltpu.VMEM((COL, 2, 2, big // 2, cols), bf),
-            pltpu.VMEM((LAND_SLOTS, 2, 2, big, cols), bf),
-            pltpu.VMEM((COL, 2, 2, small // 2, cols), bf),
-            pltpu.VMEM((COL, 2, 2, small, cols), bf),
-            pltpu.VMEM((2, small, d), bf),
-            pltpu.SemaphoreType.DMA((COL, 2, 2, 8)),
-            pltpu.SemaphoreType.DMA((COL, 2, 2, 8)),
-            pltpu.SemaphoreType.DMA((8,)),
-            pltpu.SemaphoreType.DMA((8,)),
-            pltpu.SemaphoreType.DMA((6,)),
+            pltpu.VMEM((n_chunk, d // depth, TPA, TPA, depth // TPA // TPA, hd), bf),
+            pltpu.VMEM((seq, hd), bf),
+            pltpu.VMEM((2, TPA, TPA, seq // TPA // TPA, hd), bf),
+            pltpu.VMEM((seq, hd // 2), f32),
+            pltpu.VMEM((seq, hd // 2), f32),
+            pltpu.VMEM((1, d), f32),
+            pltpu.VMEM((X_SLOTS, LN_ROWS, d), bf),
+            pltpu.VMEM((QB, seq), f32),
+            pltpu.VMEM((seq, hd + ff), bf),
+            pltpu.VMEM((2, hd + ff, cols), bf),
+            dma((n_chunk, 8)),
+            dma((n_chunk, 8)),
+            dma((8,)),
+            dma((8,)),
+            dma((n_chunk, 2)),
+            dma,
+            dma((X_SLOTS,)),
+            dma((16, 4)),
+            dma((16, 4)),
+            dma((COL, 2, 2, 8)),
+            dma((COL, 2, 2, 8)),
+            dma((8, 2)),
+            dma((8, 2)),
+            dma((4,)),
+            pltpu.SemaphoreType.REGULAR,
         ],
-        compiler_params=pltpu.CompilerParams(collective_id=1, has_side_effects=True, vmem_limit_bytes=40 * 1024 * 1024),
-        cost_estimate=pl.CostEstimate(flops=2 * seq * kk * d, bytes_accessed=4 * seq * d, transcendentals=0),
-        name="down_reduce",
-    )(az, pre, x, wo, wd)
-    return write_out(res)[None]
+        compiler_params=pltpu.CompilerParams(collective_id=0, has_side_effects=True, vmem_limit_bytes=VMEM_LIMIT),
+        cost_estimate=pl.CostEstimate(flops=flops, bytes_accessed=4 * seq * d, transcendentals=0),
+        name="decoder_layer",
+    )(x, positions.reshape(seq // 128, 128), inv_freq.reshape(1, hd // 2), norm_gain.reshape(1, depth),
+      *(w.reshape(TPA, TPA, depth // TPA // TPA, w.shape[1]) for w in (w_query, w_key, w_value, w_gate, w_up)), w_out, w_down)
 
 
 def write_kernel(src, dst, sem):
-    n, seq, cols = src.shape
-    copies = [pltpu.make_async_copy(src.at[b], dst.at[:, pl.ds(b * cols, cols)], sem.at[b]) for b in range(n)]
+    parts = sem.shape[0]
+    rows = src.shape[0] // parts
+    copies = [pltpu.make_async_copy(src.at[pl.ds(b * rows, rows)], dst.at[pl.ds(b * rows, rows)], sem.at[b]) for b in range(parts)]
     for c in copies:
         c.start()
     for c in copies:
         c.wait()
 
 
-def write_out(blocks):
-    n, seq, cols = blocks.shape
+def write_out(block):
     return pl.pallas_call(
         write_kernel,
-        out_shape=jax.ShapeDtypeStruct((seq, n * cols), blocks.dtype),
+        out_shape=jax.ShapeDtypeStruct(block.shape, block.dtype),
         in_specs=[pl.BlockSpec(memory_space=pltpu.VMEM)],
         out_specs=pl.BlockSpec(memory_space=pl.ANY),
-        scratch_shapes=[pltpu.SemaphoreType.DMA((n,))],
+        scratch_shapes=[pltpu.SemaphoreType.DMA((8,))],
         compiler_params=pltpu.CompilerParams(vmem_limit_bytes=24 * 1024 * 1024),
         name="write_out",
-    )(blocks)
+    )(block)
 
 
 def solution(mesh):
     row_spec = P(("dp", "fsdp"), None, None)
 
     def local_layer(hidden, positions, norm_gain, w_query, w_key, w_value, w_gate, w_up, w_out, w_down):
-        az, pre = project_call(hidden[0], positions, norm_gain, w_query, w_key, w_value, w_gate, w_up, w_out, w_down)
-        return reduce_call(az, pre, hidden[0], w_out, w_down)
+        rows, _ = layer_call(hidden[0], positions, norm_gain, w_query, w_key, w_value, w_gate, w_up, w_out, w_down)
+        return write_out(rows)[None]
 
     in_specs = (row_spec, P(None), P("fsdp"), P("fsdp", "tp"), P("fsdp", None), P("fsdp", None), P("fsdp", "tp"), P("fsdp", "tp"), P("tp", "fsdp"), P("tp", "fsdp"))
     return jax.shard_map(local_layer, mesh=mesh, in_specs=in_specs, out_specs=row_spec, check_vma=False)

time: 299 us -> 297 us (level)
    pallas_call x3 -> x2, Pallas kernels: 298 us -> 297 us  [the longest x1 291 us: layer_call(): pl.pallas_call(layer_kernel, out_shape=(pltpu.VMEM((seq, d), bf), jax.Sha...]
where the time goes in v6:
time: 297 us
  Pallas kernels  297 us (100%)
    pallas_call x1, Pallas kernels, layer_call(): pl.pallas_call(layer_kernel, out_shape=(pltpu.VMEM((seq, d), bf), jax.Sha...  291 us

profile of v6, /device:TPU:0, one launch (start us, length us, event | category | flops | bytes accessed | tf_op | source)
XLA Modules:
  0.0 296.8 jit_solution(13243195881034418760)
XLA Ops:
  0.0 290.7 %decoder_layer.1 = (bf16[2048,4096]{1,0:T(8,128)(2,1)S(1)}, bf16[8,1280,512]{2,1,0:T(8,128)(2,1)}) custom-call(bf16[2048,4096]{1,0:T(8,128)(2,1)} %bitcast.9, s32[16,128]{1,0:T(8,128)} %bitcast.15, f32[1,128]{1,0:T(1,128)} %constant.4.inv_freq, f32[1,512]{1,0:T(1,128)} %bitcast.16, bf16[4,4,32,256]{3,2,1,0:T(8,128)(2,1)} %bitcast.12, ...), custom_call_target="tpu_custom_call" | custom-call | flops 70866960384 | bytes 33554432 | tf_op jit(solution)/shard_map/decoder_layer/pallas_call | solution.py:647
  290.7 5.9 %write_out.1 = bf16[2048,4096]{1,0:T(8,128)(2,1)} custom-call(bf16[2048,4096]{1,0:T(8,128)(2,1)S(1)} %get-tuple-element.6.src), custom_call_target="tpu_custom_call" | custom-call | tf_op jit(solution)/shard_map/write_out/pallas_call | solution.py:697

commit v7 on v6

--- a/solution.py
+++ b/solution.py
@@ -329,17 +329,16 @@
             keys_values()
             kv_start(4)
 
-        for step in range(4, 7):
-            @pl.when(j == step - 1)
-            def _(step=step):
-                kv_finish(step)
-                kv_start(step + 1)
-
-        @pl.when(j == n_x - 3)
+        @pl.when(j == 3)
+        def _():
+            kv_finish(5)
+            kv_start(6)
+
+        @pl.when(j == 4)
         def _():
             kv_finish(7)
 
-        for lo, hi, step in ((0, 5, n_x - 3), (5, 8, n_x - 2)):
+        for lo, hi, step in ((0, 3, 4), (3, 5, 5), (5, 7, 6), (7, 8, 7)):
             @pl.when(j == step)
             def _(lo=lo, hi=hi):
                 for b in range(lo, hi):
@@ -347,6 +346,16 @@
 
         ready(chunk_of(j))
         compute(chunk_of(j))
+
+        @pl.when(j == 2)
+        def _():
+            kv_finish(4)
+            kv_start(5)
+
+        @pl.when(j == 3)
+        def _():
+            kv_finish(6)
+            kv_start(7)
 
 
 def reduce_part(az, x_hbm, wo, wd, out, w2, wbuf, wvm, xb, ssem, rsem, wss, wrs, lsem, xsem, phase):
@@ -603,23 +612,24 @@
         for c in ld_x:
             c.wait()
 
-        @pl.loop(0, COL + len(stages) - 1)
+        @pl.loop(0, COL + GAP + len(stages) - 1)
         def _(n):
             for s, fn in enumerate(stages):
-                cb = n - s
-
-                @pl.when(jnp.logical_and(cb >= 0, cb < COL))
-                def _(fn=fn, cb=cb):
-                    fn(cb)
-
-            @pl.when(n + 1 < COL)
+                turn = n - s
+
+                @pl.when(jnp.logical_or(jnp.logical_and(turn >= 0, turn < 2), jnp.logical_and(turn >= 2 + GAP, turn < COL + GAP)))
+                def _(fn=fn, turn=turn):
+                    fn(jnp.where(turn >= 2, turn - GAP, turn))
+
+            @pl.when(jnp.logical_or(n < 1, jnp.logical_and(n >= 1 + GAP, n + 1 < COL + GAP)))
             def _():
-                fetch(n + 1)
+                fetch(jnp.where(n >= 1, n - GAP, n) + 1)
 
     return send_late, reduce_all
 
 
 MT = 512
+GAP = 1
 PART_SLOTS = 5
 LAND_SLOTS = 4
 

time: 297 us -> 297 us (level)
  no operation moved by 1% of the time
where the time goes in v7:
time: 297 us
  Pallas kernels  297 us (100%)
    pallas_call x1, Pallas kernels, layer_call(): pl.pallas_call(layer_kernel, out_shape=(pltpu.VMEM((seq, d), bf), jax.Sha...  291 us

profile of v7, /device:TPU:0, one launch (start us, length us, event | category | flops | bytes accessed | tf_op | source)
XLA Modules:
  0.0 297.1 jit_solution(12229452536526110865)
XLA Ops:
  0.0 291.0 %decoder_layer.1 = (bf16[2048,4096]{1,0:T(8,128)(2,1)S(1)}, bf16[8,1280,512]{2,1,0:T(8,128)(2,1)}) custom-call(bf16[2048,4096]{1,0:T(8,128)(2,1)} %bitcast.9, s32[16,128]{1,0:T(8,128)} %bitcast.15, f32[1,128]{1,0:T(1,128)} %constant.4.inv_freq, f32[1,512]{1,0:T(1,128)} %bitcast.16, bf16[4,4,32,256]{3,2,1,0:T(8,128)(2,1)} %bitcast.12, ...), custom_call_target="tpu_custom_call" | custom-call | flops 70866960384 | bytes 33554432 | tf_op jit(solution)/shard_map/decoder_layer/pallas_call | solution.py:657
  291.0 5.9 %write_out.1 = bf16[2048,4096]{1,0:T(8,128)(2,1)} custom-call(bf16[2048,4096]{1,0:T(8,128)(2,1)S(1)} %get-tuple-element.6.src), custom_call_target="tpu_custom_call" | custom-call | tf_op jit(solution)/shard_map/write_out/pallas_call | solution.py:707

commit v8 on v7

--- a/solution.py
+++ b/solution.py
@@ -271,9 +271,10 @@
                 rows = pl.ds(pl.multiple_of(m * M1, M1), M1)
                 q[rows, :] = rope(product(i, rows), rows)
 
+    def gate_up(i, lo, hi):
         @pl.when(i >= 3)
         def _():
-            for m in range(seq // M2):
+            for m in range(lo, hi):
                 rows = pl.ds(m * M2, M2)
                 y = product(i, rows)
                 g = y[:, :GU].astype(jnp.bfloat16).astype(jnp.float32)
@@ -316,7 +317,9 @@
         def _():
             net_a(j + 1)
 
-        net_b(j)
+        @pl.when(j < n_x - 1)
+        def _():
+            net_b(j)
 
         @pl.when(j == 1)
         def _():
@@ -346,6 +349,14 @@
 
         ready(chunk_of(j))
         compute(chunk_of(j))
+        n_tile = seq // M2
+        gate_up(chunk_of(j), 0, n_tile - 1)
+
+        @pl.when(j == n_x - 2)
+        def _():
+            net_b(n_x - 1)
+
+        gate_up(chunk_of(j), n_tile - 1, n_tile)
 
         @pl.when(j == 2)
         def _():

time: 297 us -> 297 us (level)
  no operation moved by 1% of the time
where the time goes in v8:
time: 297 us
  Pallas kernels  296 us (100%)
    pallas_call x1, Pallas kernels, layer_call(): pl.pallas_call(layer_kernel, out_shape=(pltpu.VMEM((seq, d), bf), jax.Sha...  291 us

profile of v8, /device:TPU:0, one launch (start us, length us, event | category | flops | bytes accessed | tf_op | source)
XLA Modules:
  0.0 296.6 jit_solution(8839833097023362842)
XLA Ops:
  0.0 290.6 %decoder_layer.1 = (bf16[2048,4096]{1,0:T(8,128)(2,1)S(1)}, bf16[8,1280,512]{2,1,0:T(8,128)(2,1)}) custom-call(bf16[2048,4096]{1,0:T(8,128)(2,1)} %bitcast.9, s32[16,128]{1,0:T(8,128)} %bitcast.15, f32[1,128]{1,0:T(1,128)} %constant.4.inv_freq, f32[1,512]{1,0:T(1,128)} %bitcast.16, bf16[4,4,32,256]{3,2,1,0:T(8,128)(2,1)} %bitcast.12, ...), custom_call_target="tpu_custom_call" | custom-call | flops 70866960384 | bytes 33554432 | tf_op jit(solution)/shard_map/decoder_layer/pallas_call | solution.py:668
  290.6 5.9 %write_out.1 = bf16[2048,4096]{1,0:T(8,128)(2,1)} custom-call(bf16[2048,4096]{1,0:T(8,128)(2,1)S(1)} %get-tuple-element.6.src), custom_call_target="tpu_custom_call" | custom-call | tf_op jit(solution)/shard_map/write_out/pallas_call | solution.py:718
